TPU v7x, 256 devices: a whole 4x4x8 slice. The times are simulated.
256 devices in a mesh: grp: 128 (over z, x, y), rep: 2 (over core).
Axes of the slice: x: 4, y: 4, z: 8, core: 2. Of those that a mesh axis runs over, the one named last changes fastest.
Arguments:
- vectors: bfloat16 [32768, 768], P(('grp', 'rep')), may hold values from -6 to 6
- list_ids: int32 [32768, 8], P(('grp', 'rep')), may hold values from -1 to 65535, as said below
- spill_weight: int32 [32768, 8], P(('grp', 'rep')), may hold values from 1 to 4
- list_pos: int32 [65536], replicated, may hold values from 0 to 65535, as said below
- old_centroids: float32 [65536, 768], P('grp'), may hold values from -12 to 12
Outputs:
- refined: float32 [65536, 768], P('grp')
- new_dist: float32 [32768, 8], P(('grp', 'rep'))
Inputs may be any that keep to these rules, and one draw needn't show every extreme that they name: `list_ids`: entries are list numbers or -1; the lists of one row are distinct. List l is owned by grp index list_pos[l] // 512. Among the rows of one device (aligned blocks of 128 rows), at most 4 slots name lists of one owner, and in every block some owner gets exactly 4. `list_pos`: A permutation of the list numbers.
All inputs are finite; a program needn't handle non-finite values.
Results may differ from a plain program's by a relative error of at most 0.0003.
Values may be sent and summed in bfloat16 or wider, within the bound.
No kernel may reach another device: no remote copies, remote signals or barrier semaphores. Data moves between devices by JAX's collectives and lax.ppermute only.
A program may use at most 64 MiB of HBM per device.

v0:
```python
import math

import jax
import jax.numpy as jnp
from jax import lax
from jax.sharding import PartitionSpec as P

D = 768


def side_by_side(arrays, axis, split_dim, concat_dim, along):
    both = jnp.concatenate(arrays, axis=along)
    result, at, finished = (
        lax.all_to_all(both, axis, split_axis=split_dim, concat_axis=concat_dim, tiled=True),
        0,
        [],
    )
    for a in arrays:
        finished.append(lax.slice_in_dim(result, at, at + a.shape[along], axis=along))
        at += a.shape[along]
    return tuple(finished)


def split_up(value, dim, size):
    before, after = (value.shape[:dim], value.shape[dim + 1 :])
    return jnp.moveaxis(value.reshape(*before, size, -1, *after), dim, 0)


def sum_at_owner(value, axis, dim):
    pieces = split_up(value, dim, lax.axis_size(axis))
    arrived = lax.all_to_all(pieces, axis, split_axis=0, concat_axis=0, tiled=True)
    return arrived.sum(axis=0)


def in_one_piece(arrays, axis, dim, along):
    widths = [math.prod(a.shape[along:]) for a in arrays]
    both = jnp.concatenate(
        [a.reshape(*a.shape[:along], w) for a, w in zip(arrays, widths)], axis=along
    )
    result = sum_at_owner(both, axis, dim)
    pieces = jnp.split(result, [sum(widths[:k]) for k in range(1, len(widths))], axis=along)
    return tuple(
        (b.reshape(*result.shape[:along], *a.shape[along:]) for a, b in zip(arrays, pieces))
    )


def from_everyone(value, axis):
    size = lax.axis_size(axis)
    return lax.all_to_all(
        jnp.broadcast_to(value[None], (size, *value.shape)), axis, 0, 0, tiled=True
    )


def joined_along(pieces, dim):
    pieces = jnp.moveaxis(pieces, 0, dim)
    dims = pieces.shape
    return pieces.reshape(*dims[:dim], dims[dim] * dims[dim + 1], *dims[dim + 2 :])


def collect(value, axis, dim):
    pieces = from_everyone(value, axis)
    return joined_along(pieces, dim)


def decode_meta(meta_rows):
    values = meta_rows.astype(jnp.int32)
    tag_value = values[:, 0] * 128 + values[:, 1]
    return (tag_value > 0, jnp.maximum(tag_value - 1, 0), values[:, 2].astype(jnp.float32))


def pick_block(table, index_block):
    table_iota = jnp.arange(table.shape[0], dtype=jnp.int32)
    if table.dtype == jnp.float32:
        selector = (index_block[:, None] == table_iota[None, :]).astype(jnp.float32)
        return jnp.dot(
            selector, table, precision=lax.Precision.HIGHEST, preferred_element_type=jnp.float32
        )
    selector = (index_block[:, None] == table_iota[None, :]).astype(table.dtype)
    return jnp.dot(selector, table, preferred_element_type=jnp.float32).astype(table.dtype)


def pick_rows(table, indices):
    total_rows = indices.shape[0]
    block_rows = math.gcd(512, total_rows)
    block_count = total_rows // block_rows
    picked = lax.map(
        lambda index_block: pick_block(table, index_block), indices.reshape(block_count, block_rows)
    )
    return picked.reshape(total_rows, table.shape[1])


def owner_sums(rows_all, slot_all, weight_all, old_centroids, lists_here):
    total_rows, feature_dim = rows_all.shape
    block_rows = math.gcd(512, total_rows)
    block_count = total_rows // block_rows
    row_blocks = rows_all.reshape(block_count, block_rows, feature_dim)
    slot_blocks = slot_all.reshape(block_count, block_rows)
    weight_blocks = weight_all.reshape(block_count, block_rows)
    list_iota = jnp.arange(lists_here, dtype=jnp.int32)

    def accumulate(running, piece_item):
        weighted_sums, totals = running
        rows_in, slot_in, weight_in = piece_item
        row_values = rows_in.astype(jnp.float32)
        centre_rows = pick_block(old_centroids, slot_in)
        sq_norms = jnp.sum((row_values - centre_rows) ** 2, axis=-1)
        shares = weight_in / (1.0 + sq_norms / D)
        placed = (slot_in[None, :] == list_iota[:, None]).astype(jnp.float32) * shares[None, :]
        weighted_sums = weighted_sums + jnp.dot(
            placed, row_values, precision=lax.Precision.HIGHEST, preferred_element_type=jnp.float32
        )
        totals = totals + jnp.sum(placed, axis=1)
        return ((weighted_sums, totals), jnp.float32(0.0))

    start_state = (
        jnp.zeros((lists_here, feature_dim), jnp.float32),
        jnp.zeros((lists_here,), jnp.float32),
    )
    final_state, unused = lax.scan(
        accumulate, start_state, (row_blocks, slot_blocks, weight_blocks)
    )
    return final_state


def shards(vectors, list_ids, spill_weight, list_pos, old_centroids):
    owners = lax.axis_size("grp")
    row_count, slot_count = list_ids.shape
    feature_dim = vectors.shape[1]
    lists_here = old_centroids.shape[0]
    cap_slots = row_count * slot_count // (2 * owners)
    seat_total = owners * cap_slots
    pair_count = row_count * slot_count
    is_live = list_ids >= 0
    places = jnp.where(is_live, list_pos[jnp.maximum(list_ids, 0)], 0)
    target = jnp.where(is_live, places // lists_here, owners).reshape(-1)
    sorted_order = jnp.argsort(target, stable=True)
    ranked = target[sorted_order]
    counts = jnp.sum(
        (target[:, None] == jnp.arange(owners, dtype=jnp.int32)[None, :]).astype(jnp.int32), axis=0
    )
    starts = jnp.concatenate([jnp.cumsum(counts) - counts, jnp.zeros((1,), jnp.int32)])
    within = jnp.arange(pair_count, dtype=jnp.int32) - starts[ranked]
    seat_sorted = jnp.where(ranked < owners, ranked * cap_slots + within, seat_total)
    seat_index = jnp.zeros((pair_count,), jnp.int32).at[sorted_order].set(seat_sorted)
    pair_of_seat = (
        jnp.full((seat_total,), -1, jnp.int32)
        .at[seat_index]
        .set(jnp.arange(pair_count, dtype=jnp.int32), mode="drop")
    )
    filled = pair_of_seat >= 0
    pair_safe = jnp.maximum(pair_of_seat, 0)
    source_row = jnp.where(filled, pair_safe // slot_count, -1)
    send_rows = pick_rows(vectors, source_row)
    local_flat = (places % lists_here).reshape(-1)
    weight_flat = spill_weight.reshape(-1)
    tag_out = jnp.where(filled, local_flat[pair_safe] + 1, 0)
    weight_out = jnp.where(filled, weight_flat[pair_safe], 0)
    send_meta = jnp.stack([tag_out // 128, tag_out % 128, weight_out], axis=-1).astype(jnp.bfloat16)
    got_rows, got_meta = side_by_side(
        (
            send_rows.reshape(owners, cap_slots, feature_dim),
            send_meta.reshape(owners, cap_slots, 3),
        ),
        "grp",
        0,
        0,
        2,
    )
    got_rows = got_rows.reshape(seat_total, feature_dim)
    got_meta = got_meta.reshape(seat_total, 3)
    seat_live, seat_row, seat_weight = decode_meta(got_meta)
    weighted_sums, totals = owner_sums(got_rows, seat_row, seat_weight, old_centroids, lists_here)
    half_sums, half_totals = in_one_piece((weighted_sums, totals), "rep", 0, 1)
    part_rows = half_sums.shape[0]
    first_row = lax.axis_index("rep") * part_rows
    mine = lax.dynamic_slice_in_dim(old_centroids, first_row, part_rows, 0)
    refined = collect((mine + half_sums) / (1.0 + half_totals[:, None]), "rep", 0)
    block_rows = math.gcd(512, seat_total)
    block_count = seat_total // block_rows
    row_blocks = got_rows.reshape(block_count, block_rows, feature_dim)
    slot_blocks = seat_row.reshape(block_count, block_rows)

    def distance(piece_item):
        rows_in, slot_in = piece_item
        row_values = rows_in.astype(jnp.float32)
        return jnp.sum((row_values - pick_block(refined, slot_in)) ** 2, axis=-1) / D

    owner_dist = lax.map(distance, (row_blocks, slot_blocks)).reshape(owners, cap_slots)
    seat_dist = lax.all_to_all(owner_dist, "grp", split_axis=0, concat_axis=0, tiled=True).reshape(
        seat_total
    )
    picked = seat_dist[jnp.minimum(seat_index, seat_total - 1)].reshape(row_count, slot_count)
    new_dist = jnp.where(is_live, picked, jnp.float32(0.0))
    return (refined, new_dist)


def solution(mesh):
    return jax.shard_map(
        shards,
        mesh=mesh,
        in_specs=(
            P(("grp", "rep"), None),
            P(("grp", "rep"), None),
            P(("grp", "rep"), None),
            P(),
            P("grp", None),
        ),
        out_specs=(P("grp", None), P(("grp", "rep"), None)),
        check_vma=False,
    )
```

profile of v0, /device:TPU:1, one launch (start us, length us, event | category | flops | bytes accessed | tf_op | source)
XLA Modules:
  0.0 140.8 jit_solution(3350607121231050002)
XLA Ops:
  1.7 6.1 %gather_fusion = s32[1024]{0:T(1024)S(1)} fusion(s32[65536]{0:T(1024)S(1)} %copy-done.1, s32[1024]{0:T(1024)S(1)} %broadcast_clamp_fusion.2), kind=kCustom, calls=%fused_computation | custom fusion | bytes 12288 | tf_op jit(solution)/shard_map/gather | solution.py:134
  8.8 4.4 %sort.17 = (s32[1024]{0:T(1024)}, s32[1024]{0:T(1024)S(1)}) sort(s32[1024]{0:T(1024)S(1)} %reshape.164, s32[1024]{0:T(1024)S(1)} %iota.33), dimensions={0}, to_apply=%region_0.1 | sort | flops 10240 | bytes 16384 | tf_op jit(solution)/shard_map/jit(argsort)/sort | solution.py:136
  13.2 4.5 %gather_fusion.1 = s32[1024]{0:T(1024)S(1)} fusion(s32[1024]{0:T(1024)S(1)} %reshape.164, s32[1024]{0:T(1024)S(1)} %get-tuple-element.75), kind=kCustom, calls=%fused_computation.1 | custom fusion | bytes 12288 | tf_op jit(solution)/shard_map/gather | solution.py:137
  17.8 6.8 %gather_fusion.2 = s32[1024]{0:T(1024)S(1)} fusion(s32[129]{0:T(256)S(1)} %pad_add_fusion, s32[1024]{0:T(1024)S(1)} %broadcast_clamp_fusion), kind=kCustom, calls=%fused_computation.2 | custom fusion | bytes 12288 | tf_op jit(solution)/shard_map/gather | solution.py:142
  24.6 4.3 %scatter_custom_fusion = s32[1024]{0:T(1024)S(1)} fusion(s32[1024]{0:T(1024)S(1)} %get-tuple-element.76, s32[1024]{0:T(1024)S(1)} %add_select_fusion.2, s32[]{:T(128)} %constant.129.clone.1), kind=kCustom, calls=%fused_computation.77 | custom fusion | bytes 4100 | tf_op jit(solution)/shard_map/scatter | solution.py:144
  29.5 4.3 %scatter_custom_fusion.1 = s32[512]{0:T(512)S(1)} fusion(s32[1024]{0:T(1024)S(1)} %get-tuple-element.74, s32[1024]{0:T(1024)S(1)} %iota.35, s32[]{:T(128)} %constant.131.clone.1), kind=kCustom, calls=%fused_computation.88 | custom fusion | bytes 2052 | tf_op jit(solution)/shard_map/scatter | solution.py:148
  34.2 2.3 %gather_fusion.3 = s32[512]{0:T(512)S(1)} fusion(s32[1024]{0:T(1024)S(1)} %reshape.167, s32[1024]{0:T(1024)S(1)} %pad_clamp_fusion), kind=kCustom, calls=%fused_computation.3 | custom fusion | bytes 6144 | tf_op jit(solution)/shard_map/gather | solution.py:156
  36.5 2.3 %gather_fusion.4 = s32[512]{0:T(512)S(1)} fusion(s32[1024]{0:T(1024)S(1)} %reshape.168, s32[1024]{0:T(1024)S(1)} %pad_clamp_fusion), kind=kCustom, calls=%fused_computation.4 | custom fusion | bytes 6144 | tf_op jit(solution)/shard_map/gather | solution.py:157
  40.2 1.6 %pad_maximum_fusion.1 = bf16[128,4,771]{2,1,0:T(4,128)(2,1)} fusion(bf16[128,4,1]{2,1,0:T(4,128)(2,1)S(1)} %stack.15, bf16[128,4,1]{2,1,0:T(4,128)(2,1)S(1)} %stack.14, bf16[128,4,1]{2,1,0:T(4,128)(2,1)S(1)} %stack.13, bf16[128,4,768]{2,1,0:T(4,128)(2,1)S(1)} %reshape_reshape.2), kind=kLoop, calls=%fused_computation.22 | loop fusion | flops 3158016 | bytes 1579008 | tf_op jit(solution)/shard_map/concatenate | solution.py:12
  41.8 16.5 %all-to-all-start = ((bf16[128,4,771]{2,1,0:T(4,128)(2,1)}), bf16[128,4,771]{2,1,0:T(4,128)(2,1)S(1)}, u32[]{:S(2)}, u32[]{:S(2)}) async-start(bf16[128,4,771]{2,1,0:T(4,128)(2,1)} %pad_maximum_fusion.1), calls=%async_computation | async-start | bytes 1835008 | tf_op jit(solution)/shard_map/all_to_all | solution.py:14
  58.4 1.2 copy.85
  59.6 24.8 %all-to-all-done = bf16[128,4,771]{2,1,0:T(4,128)(2,1)S(1)} async-done(((bf16[128,4,771]{2,1,0:T(4,128)(2,1)}), bf16[128,4,771]{2,1,0:T(4,128)(2,1)S(1)}, u32[]{:S(2)}, u32[]{:S(2)}) %all-to-all-start) | async-done | bytes 789536 | tf_op jit(solution)/shard_map/all_to_all | solution.py:14
  84.7 1.1 squeeze.20
  85.8 1.1 reshape.245
  87.3 2.9 %fusion.1 = f32[512]{0:T(512)S(1)} fusion(bf16[512,768]{1,0:T(8,128)(2,1)} %squeeze.20, f32[512,768]{1,0:T(8,128)S(1)} %copy-done, s32[512]{0:T(512)S(1)} %bitcast.18), kind=kOutput, calls=%fused_computation.12 | convolution fusion | flops 2417753600 | bytes 2363392 | tf_op jit(solution)/shard_map/while/body/eval_jaxpr/dot_general | solution.py:75
  91.4 1.5 %fusion.4 = f32[2,256,768]{2,1,0:T(8,128)S(1)} fusion(bf16[512,768,1]{1,0,2:T(8,128)(2,1)S(1)} %copy-done.2, f32[512]{0:T(512)S(1)} %add_divide_fusion, s32[2,256]{1,0:T(2,128)S(1)} %multiply_add_fusion, s32[512]{0:T(512)S(1)} %bitcast.20), kind=kOutput, calls=%fused_computation.18 | convolution fusion | flops 2416443392 | bytes 2365440 | tf_op jit(solution)/shard_map/while/body/eval_jaxpr/dot_general | solution.py:109
  93.1 1.6 %copy.81 = f32[2,256,769]{1,2,0:T(8,128)} copy(f32[2,256,769]{2,1,0:T(8,128)S(1)} %pad_maximum_fusion) | data formatting | bytes 3149824 | tf_op jit(solution)/shard_map/concatenate | solution.py:37
  94.7 9.0 %all_to_all.21 = f32[2,256,769]{1,2,0:T(8,128)S(1)} all-to-all(f32[2,256,769]{1,2,0:T(8,128)} %copy.81), channel_id=1, replica_groups=mesh['grp'=128,'rep'=2] {'rep'}, dimensions={0} | all-to-all | bytes 3149824 | tf_op jit(solution)/shard_map/all_to_all | solution.py:31
  105.4 1.5 %fusion.7 = f32[256,768]{0,1:T(8,128)S(1)} fusion(f32[256,768]{0,1:T(8,128)} %copy.85, f32[256,769]{0,1:T(8,128)} %reduce_sum.51, f32[256]{0:T(256)S(1)} %bitcast.24), kind=kLoop, calls=%fused_computation.24 | loop fusion | flops 393216 | bytes 2360320 | tf_op jit(solution)/shard_map/div | solution.py:177
  107.3 5.1 %all_to_all.22 = f32[2,256,768]{2,1,0:T(8,128)S(1)} all-to-all(f32[2,256,768]{2,1,0:T(8,128)S(1)} %broadcast_in_dim.82), channel_id=1, replica_groups=mesh['grp'=128,'rep'=2] {'rep'}, dimensions={0} | all-to-all | bytes 3145728 | tf_op jit(solution)/shard_map/all_to_all | solution.py:49
  112.4 1.7 %fusion.3 = f32[512]{0:T(512)S(1)} fusion(bf16[512,768]{1,0:T(8,128)(2,1)S(1)} %copy-done.4, f32[512,768]{1,0:T(8,128)S(1)} %bitcast.14, s32[512]{0:T(512)S(1)} %bitcast.21), kind=kOutput, calls=%fused_computation.14 | convolution fusion | flops 2417753600 | bytes 2363392 | tf_op jit(solution)/shard_map/while/body/eval_jaxpr/dot_general | solution.py:75
  114.3 16.3 %all_to_all.23 = f32[128,1,4]{2,1,0:T(1,128)S(1)} all-to-all(f32[128,1,4]{2,1,0:T(1,128)S(1)} %bitcast.16), channel_id=1, replica_groups=mesh['grp'=128,'rep'=2] {'grp'}, dimensions={0} | all-to-all | bytes 4096 | tf_op jit(solution)/shard_map/all_to_all | solution.py:189
  132.0 6.9 %gather_fusion.5 = f32[1024]{0:T(1024)S(1)} fusion(f32[512]{0:T(512)S(1)} %reshape.170, s32[1024]{0:T(1024)S(1)} %copy-done.6), kind=kCustom, calls=%fused_computation.5 | custom fusion | bytes 12288 | tf_op jit(solution)/shard_map/gather | solution.py:192
  139.6 1.1 copy.88
  (73 shorter events, 10.8 us)
Async XLA Ops:
  0.6 57.7 %copy-start = (f32[512,768]{1,0:T(8,128)S(1)}, f32[512,768]{1,0:T(8,128)}, u32[]{:S(2)}) copy-start(f32[512,768]{1,0:T(8,128)} %param.9) | copy-start | bytes 4718596
  0.6 1.1 copy-start.1
  17.8 16.2 %copy-start.7 = (s32[128,8]{0,1:T(8,128)S(1)}, s32[128,8]{0,1:T(8,128)}, u32[]{:S(2)}) copy-start(s32[128,8]{0,1:T(8,128)} %param.7) | copy-start | bytes 12292
  36.5 3.1 %copy-start.5 = (bf16[128,768]{1,0:T(8,128)(2,1)S(1)}, bf16[128,768]{1,0:T(8,128)(2,1)}, u32[]{:S(2)}) copy-start(bf16[128,768]{1,0:T(8,128)(2,1)} %param.5) | copy-start | bytes 589828
  41.8 42.6 %all-to-all-start = ((bf16[128,4,771]{2,1,0:T(4,128)(2,1)}), bf16[128,4,771]{2,1,0:T(4,128)(2,1)S(1)}, u32[]{:S(2)}, u32[]{:S(2)}) async-start(bf16[128,4,771]{2,1,0:T(4,128)(2,1)} %pad_maximum_fusion.1), calls=%async_computation | async-start | bytes 1835008 | tf_op jit(solution)/shard_map/all_to_all | solution.py:14
  87.3 4.0 %copy-start.2 = (bf16[512,768,1]{1,0,2:T(8,128)(2,1)S(1)}, bf16[512,768,1]{1,0,2:T(8,128)(2,1)}, u32[]{:S(2)}) copy-start(bf16[512,768,1]{1,0,2:T(8,128)(2,1)} %reshape.245) | copy-start | bytes 2359300
  91.4 1.6 %copy-start.3 = (f32[2,256,1]{2,1,0:T(8,128)S(1)}, f32[2,256,1]{2,1,0:T(8,128)}, u32[]{:S(2)}) copy-start(f32[2,256,1]{2,1,0:T(8,128)} %concatenate.19) | copy-start | bytes 6148
  107.2 5.1 %copy-start.4 = (bf16[512,768]{1,0:T(8,128)(2,1)S(1)}, bf16[512,768]{1,0:T(8,128)(2,1)}, u32[]{:S(2)}) copy-start(bf16[512,768]{1,0:T(8,128)(2,1)} %squeeze.20) | copy-start | bytes 2359300
  112.4 19.6 %copy-start.6 = (s32[1024]{0:T(1024)S(1)}, s32[1024]{0:T(1024)}, u32[]{:S(2)}) copy-start(s32[1024]{0:T(1024)} %get-tuple-element.73) | copy-start | bytes 12292
where the time goes:
time: 141 us
  local copies, waits for them, and re-layouts  49.8 us (35%)
  blocking collectives  30.4 us (22%)
  waiting for transfers between devices  24.8 us (18%)
  starting transfers between devices  16.5 us (12%)
  other arithmetic  11.6 us (8%)
  matrix products  6.61 us (5%)
    all_to_all x1, waiting for transfers between devices, side_by_side(): lax.all_to_all(both, axis, split_axis=split_dim, concat_axis=concat_dim,...  24.8 us
    all_to_all x1, starting transfers between devices, side_by_side(): lax.all_to_all(both, axis, split_axis=split_dim, concat_axis=concat_dim,...  16.5 us
    all_to_all x1, blocking collectives, shards(): lax.all_to_all(owner_dist, 'grp', split_axis=0, concat_axis=0, tiled=True)  16.3 us
    all_to_all x1, blocking collectives, sum_at_owner(): lax.all_to_all(pieces, axis, split_axis=0, concat_axis=0, tiled=True)  8.96 us
    gather x1, local copies, waits for them, and re-layouts, shards(): seat_dist[jnp.minimum(seat_index, seat_total - 1)]  6.87 us
    gather x1, local copies, waits for them, and re-layouts, shards(): within = jnp.arange(pair_count, dtype=jnp.int32) - starts[ranked]  6.83 us
    gather x2, local copies, waits for them, and re-layouts, shards(): places = jnp.where(is_live, list_pos[jnp.maximum(list_ids, 0)], 0)  6.23 us
    all_to_all x1, blocking collectives, from_everyone(): lax.all_to_all(jnp.broadcast_to(value[None], (size, *value.shape)), axis,...  5.13 us
  transfers between devices with their start and end apart: 1, of which 1 were waited for; matrix products, arithmetic and copies ran while one was open for 1% of the time, Pallas kernels for 0%

commit v1 on v0

v1 whole, which is shorter than its diff:
```python
import jax
import jax.numpy as jnp
from jax import lax
from jax.experimental import pallas as pl
from jax.experimental.pallas import tpu as pltpu
from jax.sharding import PartitionSpec as P

LANES = 128
VMEM_LIMIT = 24 * 2**20
F32 = jnp.float32
BF16 = jnp.bfloat16


def iota(shape, dim):
    return lax.broadcasted_iota(jnp.int32, shape, dim)


def ones_where(mask):
    return jnp.where(mask, F32(1), F32(0)).astype(BF16)


def dot(a, b, contract=(1, 0)):
    return lax.dot_general(
        a, b, (((contract[0],), (contract[1],)), ((), ())), preferred_element_type=F32
    )


def pieces(value, count):
    result = []
    for _ in range(count):
        part = value.astype(BF16)
        result.append(part)
        value = value - part.astype(F32)
    return result


def route_kernel(ids_ref, weight_ref, table_ref, vectors_ref, send_ref, seat_ref, *, cap, lists_here):
    slots, rows = ids_ref.shape
    seats, width = send_ref.shape
    owners = seats // cap
    feature_dim = vectors_ref.shape[1]
    table = table_ref[...]
    digits = jnp.concatenate(
        [(table >> 8).astype(F32).astype(BF16), (table & 255).astype(F32).astype(BF16)], axis=1
    )
    ids = ids_ref[...]
    live = ids >= 0
    safe = jnp.maximum(ids, 0)
    high, low = safe >> 7, safe & 127
    row_of_table = iota((table.shape[0], rows), 0)
    picks = jnp.concatenate(
        [ones_where(row_of_table == high[k : k + 1]) for k in range(slots)], axis=1
    )
    found = dot(digits, picks, (0, 0))
    found = found[:LANES] * 256 + found[LANES:]
    lane_of_table = iota((LANES, rows), 0)
    place = jnp.concatenate(
        [
            jnp.sum(
                jnp.where(lane_of_table == low[k : k + 1], found[:, k * rows : (k + 1) * rows], 0.0),
                axis=0,
                keepdims=True,
            )
            for k in range(slots)
        ],
        axis=0,
    ).astype(jnp.int32)
    owner = jnp.where(live, place // lists_here, owners)
    code = (place % lists_here) * 8 + weight_ref[...]

    owner_iota = iota((owners, rows), 0)
    at_owner = [owner_iota == owner[k : k + 1] for k in range(slots)]
    before = ones_where(iota((rows, 2 * rows), 0) < iota((rows, 2 * rows), 1))
    counted = dot(jnp.concatenate([ones_where(m) for m in at_owner], axis=0), before)
    carried = jnp.zeros((owners, rows), F32)
    ranks = []
    for k in range(slots):
        here = counted[k * owners : (k + 1) * owners]
        rank = jnp.where(at_owner[k], here[:, :rows] + carried, 0.0)
        ranks.append(jnp.sum(rank, axis=0, keepdims=True))
        carried = carried + here[:, rows:]
    rank = jnp.concatenate(ranks, axis=0).astype(jnp.int32)
    seat = jnp.where(live, owner * cap + rank, -1)
    seat_ref[...] = seat

    seat_iota = iota((seats, rows), 0)
    taken = jnp.zeros((seats, rows), F32)
    codes = jnp.zeros((seats, rows), jnp.int32)
    for k in range(slots):
        match = seat_iota == seat[k : k + 1]
        taken = jnp.where(match, 1.0, taken)
        codes = jnp.where(match, code[k : k + 1], codes)
    taken = taken.astype(BF16)
    send_ref[:, :feature_dim] = dot(taken, vectors_ref[...]).astype(BF16)
    meta = jnp.concatenate(
        [(codes >> 6).astype(F32).astype(BF16), (codes & 63).astype(F32).astype(BF16), taken], axis=1
    )
    columns = (width - feature_dim)
    spread = ones_where(iota((3 * rows, columns), 0) // rows == iota((3 * rows, columns), 1))
    send_ref[:, feature_dim:] = dot(meta, spread).astype(BF16)


def seats_of(got_ref, lists_here, feature_dim):
    meta = got_ref[:, feature_dim:].astype(F32)
    code = (meta[:, 0:1] * 64 + meta[:, 1:2]).astype(jnp.int32)
    weight = (code & 7).astype(F32)
    chosen = ones_where(iota((got_ref.shape[0], lists_here), 1) == (code >> 3))
    return chosen, weight


def sums_of(got_ref, centroids):
    lists_here, feature_dim = centroids.shape
    chosen, weight = seats_of(got_ref, lists_here, feature_dim)
    centre = sum(dot(chosen, part) for part in pieces(centroids, 2))
    values = got_ref[...].astype(F32)
    sq_norms = jnp.sum((values[:, :feature_dim] - centre) ** 2, axis=1, keepdims=True)
    shares = weight / (1.0 + sq_norms / feature_dim)
    return sum(dot(chosen, part, (0, 0)) for part in pieces(values * shares, 2))


def own_sums_kernel(got_ref, centroids_ref, sums_ref):
    sums_ref[...] = sums_of(got_ref, centroids_ref[...])


def refine_kernel(own_sums_ref, peer_ref, got_ref, centroids_ref, refined_ref, dist_ref, *, cap):
    centroids = centroids_ref[...]
    lists_here, feature_dim = centroids.shape
    sums = own_sums_ref[...] + sums_of(peer_ref, centroids)
    totals = sums[:, feature_dim + 2 : feature_dim + 3]
    refined = (centroids + sums[:, :feature_dim]) / (1.0 + totals)
    refined_ref[...] = refined
    chosen, _ = seats_of(got_ref, lists_here, feature_dim)
    centre = sum(dot(chosen, part) for part in pieces(refined, 2))
    values = got_ref[:, :feature_dim].astype(F32)
    dist = jnp.sum((values - centre) ** 2, axis=1, keepdims=True) / feature_dim
    seats = got_ref.shape[0]
    owners = seats // cap
    spread = jnp.where(iota((seats, LANES), 0) % cap == iota((seats, LANES), 1), dist, 0.0)
    gather = ones_where(iota((owners, seats), 1) // cap == iota((owners, seats), 0))
    dist_ref[...] = sum(dot(gather, part) for part in pieces(spread, 3))


def pick_kernel(dist_ref, seat_ref, out_ref, *, cap):
    slots, rows = seat_ref.shape
    owners = dist_ref.shape[0]
    seat = seat_ref[...]
    by_rank = dist_ref[...].T[:8]
    owner_iota = iota((owners, rows), 0)
    at_owner = jnp.concatenate(
        [ones_where(owner_iota == (seat[k : k + 1] // cap)) for k in range(slots)], axis=1
    )
    found = sum(dot(part, at_owner) for part in pieces(by_rank, 3))
    rank_iota = iota((8, rows), 0)
    picked = jnp.concatenate(
        [
            jnp.sum(
                jnp.where(
                    rank_iota == seat[k : k + 1] % cap, found[:, k * rows : (k + 1) * rows], 0.0
                ),
                axis=0,
                keepdims=True,
            )
            for k in range(slots)
        ],
        axis=0,
    )
    out_ref[...] = jnp.where(seat >= 0, picked, 0.0)


def on_chip(kernel, outs, *args, name):
    whole = pl.BlockSpec(memory_space=pltpu.VMEM)
    return pl.pallas_call(
        kernel,
        out_shape=outs,
        in_specs=[whole] * len(args),
        out_specs=jax.tree.map(lambda _: whole, outs),
        compiler_params=pltpu.CompilerParams(vmem_limit_bytes=VMEM_LIMIT),
        name=name,
    )(*args)


def shards(vectors, list_ids, spill_weight, list_pos, old_centroids):
    owners = lax.axis_size("grp")
    row_count, slot_count = list_ids.shape
    lists_here, feature_dim = old_centroids.shape
    cap = row_count * slot_count // (2 * owners)
    seats = owners * cap
    width = feature_dim + LANES
    struct = jax.ShapeDtypeStruct

    send, seat = on_chip(
        lambda *refs: route_kernel(*refs, cap=cap, lists_here=lists_here),
        (struct((seats, width), BF16), struct((slot_count, row_count), jnp.int32)),
        list_ids.T,
        spill_weight.T,
        list_pos.reshape(-1, LANES),
        vectors,
        name="route",
    )
    got = lax.all_to_all(send.reshape(owners, cap, width), "grp", 0, 0, tiled=True)
    got = got.reshape(seats, width)
    peer = lax.ppermute(got, "rep", [(0, 1), (1, 0)])
    own_sums = on_chip(
        own_sums_kernel, struct((lists_here, width), F32), got, old_centroids, name="own_sums"
    )
    refined, owner_dist = on_chip(
        lambda *refs: refine_kernel(*refs, cap=cap),
        (struct((lists_here, feature_dim), F32), struct((owners, LANES), F32)),
        own_sums,
        peer,
        got,
        old_centroids,
        name="refine",
    )
    seat_dist = lax.all_to_all(owner_dist.reshape(owners, 1, LANES), "grp", 0, 0, tiled=True)
    new_dist = on_chip(
        lambda *refs: pick_kernel(*refs, cap=cap),
        struct((slot_count, row_count), F32),
        seat_dist.reshape(owners, LANES),
        seat,
        name="pick",
    )
    return refined, new_dist.T


def solution(mesh):
    return jax.shard_map(
        shards,
        mesh=mesh,
        in_specs=(
            P(("grp", "rep"), None),
            P(("grp", "rep"), None),
            P(("grp", "rep"), None),
            P(),
            P("grp", None),
        ),
        out_specs=(P("grp", None), P(("grp", "rep"), None)),
        check_vma=False,
    )
```

time: 141 us -> 78.6 us (0.56)
  local copies, waits for them, and re-layouts: 49.8 us -> 3.67 us
  blocking collectives: 30.4 us -> 58.9 us
  waiting for transfers between devices: 24.8 us -> 0.01 us
  starting transfers between devices: 16.5 us -> 3.25 us
  Pallas kernels: 0 us -> 11.9 us
  other arithmetic: 11.6 us -> 0 us
  matrix products: 6.61 us -> 0 us
    gather x7 -> x0, local copies, waits for them, and re-layouts: 29 us -> none  [the longest x1 6.87 us: shards(): seat_dist[jnp.minimum(seat_index, seat_total - 1)]]
    all_to_all x3 -> x2, blocking collectives: 30.4 us -> 58.9 us  [the longest x1 42.5 us: shards(): lax.all_to_all(send.reshape(owners, cap, width), 'grp', 0, 0, tiled=True)]
    all_to_all x1 -> x0, waiting for transfers between devices: 24.8 us -> none  [side_by_side(): lax.all_to_all(both, axis, split_axis=split_dim, concat_axis=concat_dim,...]
    all_to_all x1 -> x0, starting transfers between devices: 16.5 us -> none  [side_by_side(): lax.all_to_all(both, axis, split_axis=split_dim, concat_axis=concat_dim,...]
    pallas_call x0 -> x4, Pallas kernels: none -> 11.9 us  [on_chip(): pl.pallas_call(kernel, out_shape=outs, in_specs=[whole] * len(args), out_...]
    scatter x2 -> x0, local copies, waits for them, and re-layouts: 8.61 us -> none  [the longest x1 4.31 us: shards(): jnp.zeros((pair_count,), jnp.int32).at[sorted_order].set(seat_sorted)]
    dot_general x4 -> x0, matrix products: 6.61 us -> none  [the longest x2 4.64 us: pick_block(): jnp.dot(selector, table, precision=lax.Precision.HIGHEST, preferred_eleme...]
    sort x1 -> x0, other arithmetic: 4.37 us -> none  [shards(): sorted_order = jnp.argsort(target, stable=True)]
  transfers between devices with their start and end apart: 1 -> 1, of which waited for: 1 -> 0; matrix products, arithmetic and copies ran while one was open for 1% -> 0% of each run, Pallas kernels for 0% -> 5%
where the time goes in v1:
time: 78.6 us; the launch traced here: 78.3 us
  blocking collectives  58.9 us (75%)
  Pallas kernels  11.9 us (15%)
  local copies, waits for them, and re-layouts  3.67 us (5%)
  starting transfers between devices  3.25 us (4%)
    all_to_all x1, blocking collectives, shards(): lax.all_to_all(send.reshape(owners, cap, width), 'grp', 0, 0, tiled=True)  42.5 us
    all_to_all x1, blocking collectives, shards(): lax.all_to_all(owner_dist.reshape(owners, 1, LANES), 'grp', 0, 0, tiled=T...  16.3 us
    pallas_call x4, Pallas kernels, on_chip(): pl.pallas_call(kernel, out_shape=outs, in_specs=[whole] * len(args), out_...  11.9 us
    ppermute x1, starting transfers between devices, shards(): peer = lax.ppermute(got, 'rep', [(0, 1), (1, 0)])  3.25 us
    unnamed x10, local copies, waits for them, and re-layouts  3.25 us
  transfers between devices with their start and end apart: 1, of which 0 were waited for; matrix products, arithmetic and copies ran while one was open for 0% of the time, Pallas kernels for 5%

profile of v1, /device:TPU:1, one launch (start us, length us, event | category | flops | bytes accessed | tf_op | source)
XLA Modules:
  0.0 78.3 jit_solution(12476255942000431493)
XLA Ops:
  0.6 0.0 copy-start.1
  0.6 0.9 %copy-done.1 = s32[65536]{0:T(1024)S(1)} copy-done((s32[65536]{0:T(1024)S(1)}, s32[65536]{0:T(1024)}, u32[]{:S(2)}) %copy-start.1) | copy-done | bytes 262168
  1.6 0.0 copy-start.2
  1.6 0.9 %copy-done.2 = bf16[128,768]{1,0:T(8,128)(2,1)S(1)} copy-done((bf16[128,768]{1,0:T(8,128)(2,1)S(1)}, bf16[128,768]{1,0:T(8,128)(2,1)}, u32[]{:S(2)}) %copy-start.2) | copy-done | bytes 196632
  2.5 0.0 copy-start.3
  2.5 0.7 copy-done.3
  3.2 0.0 copy-start.4
  3.2 0.7 copy-done.4
  3.9 1.7 %route.1 = (bf16[512,896]{1,0:T(8,128)(2,1)S(1)}, s32[8,128]{1,0:T(8,128)S(1)}) custom-call(s32[8,128]{1,0:T(8,128)S(1)} %bitcast.11, s32[8,128]{1,0:T(8,128)S(1)} %bitcast.12, s32[512,128]{1,0:T(8,128)S(1)} %bitcast.8, bf16[128,768]{1,0:T(8,128)(2,1)S(1)} %copy-done.2), custom_call_target="tpu_custom_call" | custom-call | tf_op jit(solution)/shard_map/route/pallas_call | solution.py:172
  5.5 0.2 reshape.20
  5.8 0.0 copy-start
  5.8 42.5 %all_to_all.10 = bf16[128,4,896]{2,1,0:T(4,128)(2,1)S(1)} all-to-all(bf16[128,4,896]{2,1,0:T(4,128)(2,1)S(1)} %reshape.20), channel_id=1, replica_groups=mesh['grp'=128,'rep'=2] {'grp'}, dimensions={0} | all-to-all | bytes 1835008 | tf_op jit(solution)/shard_map/all_to_all | solution.py:200
  48.3 0.2 reshape.21.got_ref.refs_2_
  48.5 3.3 %collective-permute-start = (bf16[512,896]{1,0:T(8,128)(2,1)S(1)}, bf16[512,896]{1,0:T(8,128)(2,1)S(1)}, u32[]{:S(2)}, u32[]{:S(2)}) collective-permute-start(bf16[512,896]{1,0:T(8,128)(2,1)S(1)} %reshape.21.got_ref.refs_2_), channel_id=1, source_target_pairs={{0,1},{1,0},{2,3},{3,2},{4,5},{5,4},{6,7},{7,6},{8,9},{9,8},{10,11... | collective-permute-start | bytes 2752520 | tf_op jit(solution)/shard_map/ppermute | solution.py:202
  51.8 0.0 copy-done
  51.8 3.9 %own_sums.1.refs_0_ = f32[512,896]{1,0:T(8,128)S(1)} custom-call(bf16[512,896]{1,0:T(8,128)(2,1)S(1)} %reshape.21.got_ref.refs_2_, f32[512,768]{1,0:T(8,128)S(1)} %copy-done), custom_call_target="tpu_custom_call" | custom-call | tf_op jit(solution)/shard_map/own_sums/pallas_call | solution.py:172
  55.7 0.0 collective-permute-done.refs_1_
  55.7 5.4 %refine.1 = (f32[512,768]{1,0:T(8,128)}, f32[128,128]{1,0:T(8,128)S(1)}) custom-call(f32[512,896]{1,0:T(8,128)S(1)} %own_sums.1.refs_0_, bf16[512,896]{1,0:T(8,128)(2,1)S(1)} %collective-permute-done.refs_1_, bf16[512,896]{1,0:T(8,128)(2,1)S(1)} %reshape.21.got_ref.refs_2_, f32[512,768]{1,0:T(8,128)S(1)} %copy-done), custom_call_target="tpu_custom_call" | custom-call | tf_op jit(solution)/shard_map/refine/pallas_call | solution.py:172
  61.1 16.3 %all_to_all.11 = f32[128,1,128]{2,1,0:T(1,128)S(1)} all-to-all(f32[128,1,128]{2,1,0:T(1,128)S(1)} %bitcast.10), channel_id=1, replica_groups=mesh['grp'=128,'rep'=2] {'grp'}, dimensions={0} | all-to-all | bytes 131072 | tf_op jit(solution)/shard_map/all_to_all | solution.py:215
  77.4 0.9 %pick.1 = f32[8,128]{1,0:T(8,128)} custom-call(f32[128,128]{1,0:T(8,128)S(1)} %bitcast.9, s32[8,128]{1,0:T(8,128)S(1)} %get-tuple-element.9.refs_1_), custom_call_target="tpu_custom_call" | custom-call | tf_op jit(solution)/shard_map/pick/pallas_call | solution.py:172
Async XLA Ops:
  0.6 1.0 %copy-start.1 = (s32[65536]{0:T(1024)S(1)}, s32[65536]{0:T(1024)}, u32[]{:S(2)}) copy-start(s32[65536]{0:T(1024)} %param.8) | copy-start | bytes 786436
  1.6 0.9 %copy-start.2 = (bf16[128,768]{1,0:T(8,128)(2,1)S(1)}, bf16[128,768]{1,0:T(8,128)(2,1)}, u32[]{:S(2)}) copy-start(bf16[128,768]{1,0:T(8,128)(2,1)} %refs_3_.2) | copy-start | bytes 589828
  2.5 0.7 copy-start.3
  3.2 0.7 copy-start.4
  5.8 46.0 %copy-start = (f32[512,768]{1,0:T(8,128)S(1)}, f32[512,768]{1,0:T(8,128)}, u32[]{:S(2)}) copy-start(f32[512,768]{1,0:T(8,128)} %refs_3_.3) | copy-start | bytes 4718596
  48.5 7.2 %collective-permute-start = (bf16[512,896]{1,0:T(8,128)(2,1)S(1)}, bf16[512,896]{1,0:T(8,128)(2,1)S(1)}, u32[]{:S(2)}, u32[]{:S(2)}) collective-permute-start(bf16[512,896]{1,0:T(8,128)(2,1)S(1)} %reshape.21.got_ref.refs_2_), channel_id=1, source_target_pairs={{0,1},{1,0},{2,3},{3,2},{4,5},{5,4},{6,7},{7,6},{8,9},{9,8},{10,11... | collective-permute-start | bytes 2752520 | tf_op jit(solution)/shard_map/ppermute | solution.py:202

commit v2 on v1

v2 whole, which is shorter than its diff:
```python
import jax
import jax.numpy as jnp
from jax import lax
from jax.experimental import pallas as pl
from jax.experimental.pallas import tpu as pltpu
from jax.sharding import PartitionSpec as P

LANES = 128
VMEM_LIMIT = 24 * 2**20
F32 = jnp.float32
BF16 = jnp.bfloat16


def iota(shape, dim):
    return lax.broadcasted_iota(jnp.int32, shape, dim)


def ones_where(mask):
    return jnp.where(mask, F32(1), F32(0)).astype(BF16)


def dot(a, b, contract=(1, 0)):
    return lax.dot_general(
        a, b, (((contract[0],), (contract[1],)), ((), ())), preferred_element_type=F32
    )


def pieces(value, count):
    result = []
    for _ in range(count):
        part = value.astype(BF16)
        result.append(part)
        value = value - part.astype(F32)
    return result


def each(count, fn, axis):
    return jnp.concatenate([fn(k) for k in range(count)], axis=axis)


def route_kernel(
    ids_hbm, weight_hbm, table_hbm, vectors_hbm, send_ref, seat_ref, ids_ref, weight_ref, table_ref,
    vectors_ref, sems, *, cap, lists_here,
):
    copies = [
        pltpu.make_async_copy(source, target, sems.at[i])
        for i, (source, target) in enumerate(
            [(ids_hbm, ids_ref), (table_hbm, table_ref), (weight_hbm, weight_ref), (vectors_hbm, vectors_ref)]
        )
    ]
    for copy in copies:
        copy.start()
    slots, rows = ids_ref.shape
    feature_dim = vectors_ref.shape[1]
    half = cap // 2
    sent = send_ref.shape[0]
    owners = sent // half
    copies[0].wait()
    ids = ids_ref[...]
    live = ids >= 0
    safe = jnp.maximum(ids, 0)
    high, low = safe >> 7, safe & 127
    row_of_table = iota((table_ref.shape[0], rows), 0)
    picks = each(slots, lambda k: ones_where(row_of_table == high[k : k + 1]), 1)
    copies[1].wait()
    table = table_ref[...]
    digits = jnp.concatenate(
        [(table >> 8).astype(F32).astype(BF16), (table & 255).astype(F32).astype(BF16)], axis=1
    )
    found = dot(digits, picks, (0, 0))
    found = found[:LANES] * 256 + found[LANES:]
    lane_of_table = iota((LANES, rows), 0)
    place = each(
        slots,
        lambda k: jnp.sum(
            jnp.where(lane_of_table == low[k : k + 1], found[:, k * rows : (k + 1) * rows], 0.0),
            axis=0,
            keepdims=True,
        ),
        0,
    ).astype(jnp.int32)
    copies[2].wait()
    owner = jnp.where(live, place // lists_here, owners)
    code = (place % lists_here) * 8 + weight_ref[...]

    owner_iota = iota((owners, rows), 0)
    at_owner = [owner_iota == owner[k : k + 1] for k in range(slots)]
    before = ones_where(iota((rows, 2 * rows), 0) < iota((rows, 2 * rows), 1))
    counted = dot(each(slots, lambda k: ones_where(at_owner[k]), 0), before)
    carried = jnp.zeros((owners, rows), F32)
    ranks = []
    for k in range(slots):
        here = counted[k * owners : (k + 1) * owners]
        rank = jnp.where(at_owner[k], here[:, :rows] + carried, 0.0)
        ranks.append(jnp.sum(rank, axis=0, keepdims=True))
        carried = carried + here[:, rows:]
    rank = jnp.concatenate(ranks, axis=0).astype(jnp.int32)
    seat = jnp.where(live, (rank % 2) * sent + owner * half + rank // 2, -1)
    seat_ref[...] = seat

    seat_iota = iota((2 * sent, rows), 0)
    taken = jnp.zeros((2 * sent, rows), F32)
    codes = jnp.zeros((2 * sent, rows), jnp.int32)
    for k in range(slots):
        match = seat_iota == seat[k : k + 1]
        taken = jnp.where(match, 1.0, taken)
        codes = jnp.where(match, code[k : k + 1], codes)
    copies[3].wait()
    vectors = vectors_ref[...]
    taken = taken.astype(BF16)
    first = (codes >> 6).astype(F32).astype(BF16)
    second = (codes & 63).astype(F32).astype(BF16)
    for b in range(2):
        send_ref[:, b * feature_dim : (b + 1) * feature_dim] = dot(
            taken[b * sent : (b + 1) * sent], vectors
        ).astype(BF16)
    meta = jnp.concatenate([first[:sent], second[:sent], first[sent:], second[sent:]], axis=1)
    columns = send_ref.shape[1] - 2 * feature_dim
    spread = ones_where(iota((4 * rows, columns), 0) // rows == iota((4 * rows, columns), 1))
    send_ref[:, 2 * feature_dim :] = dot(meta, spread).astype(BF16)


def seat_vectors(got_ref, feature_dim):
    return each(2, lambda b: got_ref[:, b * feature_dim : (b + 1) * feature_dim], 0)


def sums_of(got_ref, centroids_high, centroids_low):
    lists_here, feature_dim = centroids_high.shape
    meta = got_ref[:, 2 * feature_dim :]
    vectors = seat_vectors(got_ref, feature_dim)
    seats = vectors.shape[0]
    columns = meta.astype(F32)
    code = each(
        2, lambda b: columns[:, 2 * b : 2 * b + 1] * 64 + columns[:, 2 * b + 1 : 2 * b + 2], 0
    ).astype(jnp.int32)
    chosen = ones_where(iota((seats, lists_here), 1) == (code >> 3))
    to_rows = ones_where(iota((8, LANES), 0) == iota((8, LANES), 1))
    rows = dot(to_rows, meta, (1, 1))
    list_row = (
        each(2, lambda b: rows[2 * b : 2 * b + 1] * 64 + rows[2 * b + 1 : 2 * b + 2], 1).astype(jnp.int32)
        >> 3
    )
    named = iota((lists_here, seats), 0) == list_row

    centre = dot(chosen, centroids_high) + dot(chosen, centroids_low)
    sq_norms = jnp.sum((vectors.astype(F32) - centre) ** 2, axis=1, keepdims=True)
    shares = (code & 7).astype(F32) / (1.0 + sq_norms / feature_dim)
    high, low = pieces(shares, 2)
    lane = iota((seats, LANES), 1)
    block = jnp.where(lane == 0, high.astype(F32), jnp.where(lane == 1, low.astype(F32), 0.0))
    share_rows = dot(to_rows, block.astype(BF16), (1, 1))
    parts = [jnp.where(named, share_rows[i : i + 1], 0.0) for i in range(2)]
    sums = sum(dot(part.astype(BF16), vectors) for part in parts)
    totals = jnp.sum(parts[0] + parts[1], axis=1, keepdims=True)
    return chosen, sums, totals


def own_sums_kernel(got_ref, centroids_ref, sums_ref, totals_ref, chosen_ref, high_ref, low_ref):
    high, low = pieces(centroids_ref[...], 2)
    high_ref[...] = high
    low_ref[...] = low
    chosen, sums, totals = sums_of(got_ref, high, low)
    chosen_ref[...] = chosen
    sums_ref[...] = sums
    totals_ref[...] = jnp.broadcast_to(totals, totals_ref.shape)


def refine_kernel(
    sums_ref, totals_ref, chosen_ref, peer_ref, got_ref, high_ref, low_ref, centroids_ref, refined_hbm,
    dist_ref, refined_ref, sem, *, cap,
):
    lists_here, feature_dim = centroids_ref.shape
    _, peer_sums, peer_totals = sums_of(peer_ref, high_ref[...], low_ref[...])
    scale = 1.0 / (1.0 + (totals_ref[:, 0:1] + peer_totals))
    refined = (centroids_ref[...] + (sums_ref[...] + peer_sums)) * scale
    refined_ref[...] = refined
    copy = pltpu.make_async_copy(refined_ref, refined_hbm, sem)
    copy.start()
    chosen = chosen_ref[...]
    centre = sum(dot(chosen, part) for part in pieces(refined, 2))
    vectors = seat_vectors(got_ref, feature_dim).astype(F32)
    dist = jnp.sum((vectors - centre) ** 2, axis=1, keepdims=True) / feature_dim
    half = cap // 2
    sent = got_ref.shape[0]
    owners = sent // half
    seat, lane = iota((2 * sent, LANES), 0), iota((2 * sent, LANES), 1)
    spread = jnp.where((seat % half) * 2 + seat // sent == lane, dist, 0.0)
    gather = ones_where((iota((owners, 2 * sent), 1) % sent) // half == iota((owners, 2 * sent), 0))
    dist_ref[...] = sum(dot(gather, part) for part in pieces(spread, 3))
    copy.wait()


def pick_kernel(dist_ref, seat_ref, out_ref, *, cap):
    slots, rows = seat_ref.shape
    owners = dist_ref.shape[0]
    half = cap // 2
    sent = owners * half
    seat = seat_ref[...]
    owner = jnp.where(seat >= 0, (seat % sent) // half, owners)
    rank = (seat % half) * 2 + seat // sent
    by_rank = dist_ref[...].T[:8]
    owner_iota = iota((owners, rows), 0)
    at_owner = each(slots, lambda k: ones_where(owner_iota == owner[k : k + 1]), 1)
    found = sum(dot(part, at_owner) for part in pieces(by_rank, 3))
    rank_iota = iota((8, rows), 0)
    picked = each(
        slots,
        lambda k: jnp.sum(
            jnp.where(rank_iota == rank[k : k + 1], found[:, k * rows : (k + 1) * rows], 0.0),
            axis=0,
            keepdims=True,
        ),
        0,
    )
    out_ref[...] = jnp.where(seat >= 0, picked, 0.0)


def on_chip(kernel, outs, *args, name, in_hbm=(), out_hbm=(), scratch=()):
    def spec(i, away):
        return pl.BlockSpec(memory_space=pltpu.HBM if i in away else pltpu.VMEM)

    args = [
        pltpu.with_memory_space_constraint(a, pltpu.HBM) if i in in_hbm else a
        for i, a in enumerate(args)
    ]

    return pl.pallas_call(
        kernel,
        out_shape=outs,
        in_specs=[spec(i, in_hbm) for i in range(len(args))],
        out_specs=[spec(i, out_hbm) for i in range(len(outs))],
        scratch_shapes=list(scratch),
        compiler_params=pltpu.CompilerParams(vmem_limit_bytes=VMEM_LIMIT),
        name=name,
    )(*args)


def shards(vectors, list_ids, spill_weight, list_pos, old_centroids):
    owners = lax.axis_size("grp")
    row_count, slot_count = list_ids.shape
    lists_here, feature_dim = old_centroids.shape
    cap = row_count * slot_count // (2 * owners)
    half = cap // 2
    sent = owners * half
    width = 2 * feature_dim + LANES
    struct = jax.ShapeDtypeStruct

    inputs = (list_ids.T, spill_weight.T, list_pos.reshape(-1, LANES), vectors)
    send, seat = on_chip(
        lambda *refs: route_kernel(*refs, cap=cap, lists_here=lists_here),
        (struct((sent, width), BF16), struct((slot_count, row_count), jnp.int32)),
        *inputs,
        name="route",
        in_hbm=range(4),
        scratch=[
            *(pltpu.VMEM(a.shape, a.dtype) for a in inputs),
            pltpu.SemaphoreType.DMA((4,)),
        ],
    )
    got = lax.all_to_all(send.reshape(owners, half, width), "grp", 0, 0, tiled=True)
    got = got.reshape(sent, width)
    peer = lax.ppermute(got, "rep", [(0, 1), (1, 0)])
    sums, totals, chosen, high, low = on_chip(
        own_sums_kernel,
        (
            struct((lists_here, feature_dim), F32),
            struct((lists_here, LANES), F32),
            struct((2 * sent, lists_here), BF16),
            struct((lists_here, feature_dim), BF16),
            struct((lists_here, feature_dim), BF16),
        ),
        got,
        old_centroids,
        name="own_sums",
    )
    refined, owner_dist = on_chip(
        lambda *refs: refine_kernel(*refs, cap=cap),
        (struct((lists_here, feature_dim), F32), struct((owners, LANES), F32)),
        sums,
        totals,
        chosen,
        peer,
        got,
        high,
        low,
        old_centroids,
        name="refine",
        out_hbm=(0,),
        scratch=[pltpu.VMEM((lists_here, feature_dim), F32), pltpu.SemaphoreType.DMA],
    )
    seat_dist = lax.all_to_all(owner_dist.reshape(owners, 1, LANES), "grp", 0, 0, tiled=True)
    (new_dist,) = on_chip(
        lambda *refs: pick_kernel(*refs, cap=cap),
        (struct((slot_count, row_count), F32),),
        seat_dist.reshape(owners, LANES),
        seat,
        name="pick",
    )
    return refined, new_dist.T


def solution(mesh):
    return jax.shard_map(
        shards,
        mesh=mesh,
        in_specs=(
            P(("grp", "rep"), None),
            P(("grp", "rep"), None),
            P(("grp", "rep"), None),
            P(),
            P("grp", None),
        ),
        out_specs=(P("grp", None), P(("grp", "rep"), None)),
        check_vma=False,
    )
```

time: 78.6 us -> 74.6 us (0.949)
  local copies, waits for them, and re-layouts: 3.67 us -> 0.65 us
  blocking collectives: 58.9 us -> 57.5 us
    unnamed x10 -> x2, local copies, waits for them, and re-layouts: 3.25 us -> 0.01 us
    all_to_all x1, blocking collectives: 42.5 us -> 41.1 us  [shards(): lax.all_to_all(send.reshape(owners, half, width), 'grp', 0, 0, tiled=True)]
  transfers between devices with their start and end apart: 1 -> 1, of which waited for: 0 -> 0; matrix products, arithmetic and copies ran while one was open for 0% -> 0% of each run, Pallas kernels for 5% -> 4%
where the time goes in v2:
time: 74.6 us; the launch traced here: 74.4 us
  blocking collectives  57.5 us (77%)
  Pallas kernels  12.2 us (16%)
  starting transfers between devices  3.37 us (5%)
    all_to_all x1, blocking collectives, shards(): lax.all_to_all(send.reshape(owners, half, width), 'grp', 0, 0, tiled=True)  41.1 us
    all_to_all x1, blocking collectives, shards(): lax.all_to_all(owner_dist.reshape(owners, 1, LANES), 'grp', 0, 0, tiled=T...  16.4 us
    pallas_call x4, Pallas kernels, on_chip(): pl.pallas_call(kernel, out_shape=outs, in_specs=[spec(i, in_hbm) for i in...  12.2 us
    ppermute x1, starting transfers between devices, shards(): peer = lax.ppermute(got, 'rep', [(0, 1), (1, 0)])  3.37 us
  transfers between devices with their start and end apart: 1, of which 0 were waited for; matrix products, arithmetic and copies ran while one was open for 0% of the time, Pallas kernels for 4%

profile of v2, /device:TPU:1, one launch (start us, length us, event | category | flops | bytes accessed | tf_op | source)
XLA Modules:
  0.0 74.4 jit_solution(12178180466435605582)
XLA Ops:
  0.6 3.0 %route.1 = (bf16[256,1664]{1,0:T(8,128)(2,1)S(1)}, s32[8,128]{1,0:T(8,128)S(1)}) custom-call(s32[8,128]{1,0:T(8,128)} %bitcast.11, s32[8,128]{1,0:T(8,128)} %bitcast.12, s32[512,128]{1,0:T(8,128)} %bitcast.10, bf16[128,768]{1,0:T(8,128)(2,1)} %refs_3_.1), custom_call_target="tpu_custom_call" | custom-call | tf_op jit(solution)/shard_map/route/pallas_call | solution.py:227
  3.6 0.3 reshape.20
  4.0 0.0 copy-start
  4.0 41.1 %all_to_all.10 = bf16[128,2,1664]{2,1,0:T(2,128)(2,1)S(1)} all-to-all(bf16[128,2,1664]{2,1,0:T(2,128)(2,1)S(1)} %reshape.20), channel_id=1, replica_groups=mesh['grp'=128,'rep'=2] {'grp'}, dimensions={0} | all-to-all | bytes 1703936 | tf_op jit(solution)/shard_map/all_to_all | solution.py:260
  45.1 0.3 reshape.21.got_ref.refs_4_
  45.5 3.4 %collective-permute-start = (bf16[256,1664]{1,0:T(8,128)(2,1)S(1)}, bf16[256,1664]{1,0:T(8,128)(2,1)S(1)}, u32[]{:S(2)}, u32[]{:S(2)}) collective-permute-start(bf16[256,1664]{1,0:T(8,128)(2,1)S(1)} %reshape.21.got_ref.refs_4_), channel_id=1, source_target_pairs={{0,1},{1,0},{2,3},{3,2},{4,5},{5,4},{6,7},{7,6},{8,9},{9,8},{10,11... | collective-permute-start | bytes 2555912 | tf_op jit(solution)/shard_map/ppermute | solution.py:262
  48.8 0.0 copy-done
  48.8 3.2 %own_sums.1 = (f32[512,768]{1,0:T(8,128)S(1)}, f32[512,128]{1,0:T(8,128)S(1)}, bf16[512,512]{1,0:T(8,128)(2,1)S(1)}, bf16[512,768]{1,0:T(8,128)(2,1)S(1)}, bf16[512,768]{1,0:T(8,128)(2,1)S(1)}) custom-call(bf16[256,1664]{1,0:T(8,128)(2,1)S(1)} %reshape.21.got_ref.refs_4_, f32[512,768]{1,0:T(8,128)S(1)} %copy-done), custom_call_target="tpu_custom_call" | custom-call | tf_op jit(solution)/shard_map/own_sums/pallas_call | solution.py:227
  52.0 0.0 collective-permute-done.refs_3_
  52.1 5.1 %refine.1 = (f32[512,768]{1,0:T(8,128)}, f32[128,128]{1,0:T(8,128)S(1)}) custom-call(f32[512,768]{1,0:T(8,128)S(1)} %get-tuple-element.12.refs_0_, f32[512,128]{1,0:T(8,128)S(1)} %get-tuple-element.13.refs_1_, bf16[512,512]{1,0:T(8,128)(2,1)S(1)} %get-tuple-element.14.refs_2_, bf16[256,1664]{1,0:T(8,128)(2,1)S(1)} %collective-permute-done.refs_3_, ...), custom_call_target="tpu_custom_call" | custom-call | tf_op jit(solution)/shard_map/refine/pallas_call | solution.py:227
  57.1 16.4 %all_to_all.11 = f32[128,1,128]{2,1,0:T(1,128)S(1)} all-to-all(f32[128,1,128]{2,1,0:T(1,128)S(1)} %bitcast.9), channel_id=1, replica_groups=mesh['grp'=128,'rep'=2] {'grp'}, dimensions={0} | all-to-all | bytes 131072 | tf_op jit(solution)/shard_map/all_to_all | solution.py:291
  73.5 0.9 %pick.1 = f32[8,128]{1,0:T(8,128)} custom-call(f32[128,128]{1,0:T(8,128)S(1)} %bitcast.8, s32[8,128]{1,0:T(8,128)S(1)} %get-tuple-element.19.refs_1_), custom_call_target="tpu_custom_call" | custom-call | tf_op jit(solution)/shard_map/pick/pallas_call | solution.py:227
Async XLA Ops:
  4.0 44.9 %copy-start = (f32[512,768]{1,0:T(8,128)S(1)}, f32[512,768]{1,0:T(8,128)}, u32[]{:S(2)}) copy-start(f32[512,768]{1,0:T(8,128)} %refs_7_.1) | copy-start | bytes 4718596
  45.5 6.6 %collective-permute-start = (bf16[256,1664]{1,0:T(8,128)(2,1)S(1)}, bf16[256,1664]{1,0:T(8,128)(2,1)S(1)}, u32[]{:S(2)}, u32[]{:S(2)}) collective-permute-start(bf16[256,1664]{1,0:T(8,128)(2,1)S(1)} %reshape.21.got_ref.refs_4_), channel_id=1, source_target_pairs={{0,1},{1,0},{2,3},{3,2},{4,5},{5,4},{6,7},{7,6},{8,9},{9,8},{10,11... | collective-permute-start | bytes 2555912 | tf_op jit(solution)/shard_map/ppermute | solution.py:262

commit v3 on v2

--- a/solution.py
+++ b/solution.py
@@ -6,6 +6,7 @@
 from jax.sharding import PartitionSpec as P
 
 LANES = 128
+CHUNK = 256
 VMEM_LIMIT = 24 * 2**20
 F32 = jnp.float32
 BF16 = jnp.bfloat16
@@ -120,69 +121,86 @@
     send_ref[:, 2 * feature_dim :] = dot(meta, spread).astype(BF16)
 
 
-def seat_vectors(got_ref, feature_dim):
-    return each(2, lambda b: got_ref[:, b * feature_dim : (b + 1) * feature_dim], 0)
-
-
-def sums_of(got_ref, centroids_high, centroids_low):
-    lists_here, feature_dim = centroids_high.shape
+def seat_vectors(got_ref, feature_dim, chunk):
+    return each(2, lambda b: got_ref[:, b * feature_dim + chunk.start : b * feature_dim + chunk.stop], 0)
+
+
+def chunks_of(feature_dim):
+    return [slice(at, at + CHUNK) for at in range(0, feature_dim, CHUNK)]
+
+
+def folded(square):
+    return sum(square[:, at : at + LANES] for at in range(0, square.shape[1], LANES))
+
+
+def own_shares_kernel(got_ref, centroids_ref, chosen_ref, rows_ref):
+    lists_here, feature_dim = centroids_ref.shape
     meta = got_ref[:, 2 * feature_dim :]
-    vectors = seat_vectors(got_ref, feature_dim)
-    seats = vectors.shape[0]
     columns = meta.astype(F32)
     code = each(
         2, lambda b: columns[:, 2 * b : 2 * b + 1] * 64 + columns[:, 2 * b + 1 : 2 * b + 2], 0
     ).astype(jnp.int32)
+    seats = code.shape[0]
     chosen = ones_where(iota((seats, lists_here), 1) == (code >> 3))
-    to_rows = ones_where(iota((8, LANES), 0) == iota((8, LANES), 1))
-    rows = dot(to_rows, meta, (1, 1))
-    list_row = (
-        each(2, lambda b: rows[2 * b : 2 * b + 1] * 64 + rows[2 * b + 1 : 2 * b + 2], 1).astype(jnp.int32)
-        >> 3
-    )
-    named = iota((lists_here, seats), 0) == list_row
-
-    centre = dot(chosen, centroids_high) + dot(chosen, centroids_low)
-    sq_norms = jnp.sum((vectors.astype(F32) - centre) ** 2, axis=1, keepdims=True)
+    chosen_ref[...] = chosen
+    total = jnp.zeros((seats, LANES), F32)
+    for chunk in chunks_of(feature_dim):
+        centre = sum(dot(chosen, part) for part in pieces(centroids_ref[:, chunk], 2))
+        total = total + folded((seat_vectors(got_ref, feature_dim, chunk).astype(F32) - centre) ** 2)
+    sq_norms = jnp.sum(total, axis=1, keepdims=True)
     shares = (code & 7).astype(F32) / (1.0 + sq_norms / feature_dim)
     high, low = pieces(shares, 2)
+    lists = code >> 3
     lane = iota((seats, LANES), 1)
     block = jnp.where(lane == 0, high.astype(F32), jnp.where(lane == 1, low.astype(F32), 0.0))
-    share_rows = dot(to_rows, block.astype(BF16), (1, 1))
-    parts = [jnp.where(named, share_rows[i : i + 1], 0.0) for i in range(2)]
-    sums = sum(dot(part.astype(BF16), vectors) for part in parts)
+    block = jnp.where(lane == 2, (lists >> 8).astype(F32), block)
+    block = jnp.where(lane == 3, (lists & 255).astype(F32), block)
+    to_rows = ones_where(iota((8, LANES), 0) == iota((8, LANES), 1))
+    rows = dot(to_rows, block.astype(BF16), (1, 1))
+    row = iota((8, seats), 0)
+    rows_ref[...] = jnp.where(row == 2, rows[2:3] * 256 + rows[3:4], rows)
+
+
+def placed(rows_ref, lists_here):
+    rows = rows_ref[...]
+    named = iota((lists_here, rows.shape[1]), 0) == rows[2:3].astype(jnp.int32)
+    parts = [jnp.where(named, rows[i : i + 1], 0.0) for i in range(2)]
     totals = jnp.sum(parts[0] + parts[1], axis=1, keepdims=True)
-    return chosen, sums, totals
-
-
-def own_sums_kernel(got_ref, centroids_ref, sums_ref, totals_ref, chosen_ref, high_ref, low_ref):
-    high, low = pieces(centroids_ref[...], 2)
-    high_ref[...] = high
-    low_ref[...] = low
-    chosen, sums, totals = sums_of(got_ref, high, low)
-    chosen_ref[...] = chosen
-    sums_ref[...] = sums
+    return [part.astype(BF16) for part in parts], totals
+
+
+def own_sums_kernel(got_ref, rows_ref, sums_ref, totals_ref):
+    lists_here, feature_dim = sums_ref.shape
+    parts, totals = placed(rows_ref, lists_here)
     totals_ref[...] = jnp.broadcast_to(totals, totals_ref.shape)
+    for chunk in chunks_of(feature_dim):
+        vectors = seat_vectors(got_ref, feature_dim, chunk)
+        sums_ref[:, chunk] = sum(dot(part, vectors) for part in parts)
 
 
 def refine_kernel(
-    sums_ref, totals_ref, chosen_ref, peer_ref, got_ref, high_ref, low_ref, centroids_ref, refined_hbm,
+    sums_ref, totals_ref, chosen_ref, peer_ref, peer_rows_ref, got_ref, centroids_ref, refined_hbm,
     dist_ref, refined_ref, sem, *, cap,
 ):
     lists_here, feature_dim = centroids_ref.shape
-    _, peer_sums, peer_totals = sums_of(peer_ref, high_ref[...], low_ref[...])
+    parts, peer_totals = placed(peer_rows_ref, lists_here)
     scale = 1.0 / (1.0 + (totals_ref[:, 0:1] + peer_totals))
-    refined = (centroids_ref[...] + (sums_ref[...] + peer_sums)) * scale
-    refined_ref[...] = refined
+    chunks = chunks_of(feature_dim)
+    for chunk in chunks:
+        vectors = seat_vectors(peer_ref, feature_dim, chunk)
+        sums = sums_ref[:, chunk] + sum(dot(part, vectors) for part in parts)
+        refined_ref[:, chunk] = (centroids_ref[:, chunk] + sums) * scale
     copy = pltpu.make_async_copy(refined_ref, refined_hbm, sem)
     copy.start()
     chosen = chosen_ref[...]
-    centre = sum(dot(chosen, part) for part in pieces(refined, 2))
-    vectors = seat_vectors(got_ref, feature_dim).astype(F32)
-    dist = jnp.sum((vectors - centre) ** 2, axis=1, keepdims=True) / feature_dim
     half = cap // 2
     sent = got_ref.shape[0]
     owners = sent // half
+    total = jnp.zeros((2 * sent, LANES), F32)
+    for chunk in chunks:
+        centre = sum(dot(chosen, part) for part in pieces(refined_ref[:, chunk], 2))
+        total = total + folded((seat_vectors(got_ref, feature_dim, chunk).astype(F32) - centre) ** 2)
+    dist = jnp.sum(total, axis=1, keepdims=True) / feature_dim
     seat, lane = iota((2 * sent, LANES), 0), iota((2 * sent, LANES), 1)
     spread = jnp.where((seat % half) * 2 + seat // sent == lane, dist, 0.0)
     gather = ones_where((iota((owners, 2 * sent), 1) % sent) // half == iota((owners, 2 * sent), 0))
@@ -259,18 +277,21 @@
     )
     got = lax.all_to_all(send.reshape(owners, half, width), "grp", 0, 0, tiled=True)
     got = got.reshape(sent, width)
-    peer = lax.ppermute(got, "rep", [(0, 1), (1, 0)])
-    sums, totals, chosen, high, low = on_chip(
-        own_sums_kernel,
-        (
-            struct((lists_here, feature_dim), F32),
-            struct((lists_here, LANES), F32),
-            struct((2 * sent, lists_here), BF16),
-            struct((lists_here, feature_dim), BF16),
-            struct((lists_here, feature_dim), BF16),
-        ),
+    swap = [(0, 1), (1, 0)]
+    peer = lax.ppermute(got, "rep", swap)
+    chosen, rows = on_chip(
+        own_shares_kernel,
+        (struct((2 * sent, lists_here), BF16), struct((8, 2 * sent), F32)),
         got,
         old_centroids,
+        name="own_shares",
+    )
+    peer_rows = lax.ppermute(rows, "rep", swap)
+    sums, totals = on_chip(
+        own_sums_kernel,
+        (struct((lists_here, feature_dim), F32), struct((lists_here, LANES), F32)),
+        got,
+        rows,
         name="own_sums",
     )
     refined, owner_dist = on_chip(
@@ -280,9 +301,8 @@
         totals,
         chosen,
         peer,
+        peer_rows,
         got,
-        high,
-        low,
         old_centroids,
         name="refine",
         out_hbm=(0,),

time: 74.6 us -> 72.5 us (0.972)
  Pallas kernels: 12.2 us -> 9.98 us
    pallas_call x4 -> x5, Pallas kernels: 12.2 us -> 9.98 us  [on_chip(): pl.pallas_call(kernel, out_shape=outs, in_specs=[spec(i, in_hbm) for i in...]
    ppermute x1 -> x2, starting transfers between devices: 3.37 us -> 3.46 us  [the longest x1 3.37 us: shards(): peer = lax.ppermute(got, 'rep', swap)]
  transfers between devices with their start and end apart: 1 -> 2, of which waited for: 0 -> 1; matrix products, arithmetic and copies ran while one was open for 0% -> 0% of each run, Pallas kernels for 4% -> 4%
where the time goes in v3:
time: 72.5 us; the launch traced here: 72.3 us
  blocking collectives  57.4 us (79%)
  Pallas kernels  9.98 us (14%)
  starting transfers between devices  3.46 us (5%)
    all_to_all x1, blocking collectives, shards(): lax.all_to_all(send.reshape(owners, half, width), 'grp', 0, 0, tiled=True)  41.1 us
    all_to_all x1, blocking collectives, shards(): lax.all_to_all(owner_dist.reshape(owners, 1, LANES), 'grp', 0, 0, tiled=T...  16.3 us
    pallas_call x5, Pallas kernels, on_chip(): pl.pallas_call(kernel, out_shape=outs, in_specs=[spec(i, in_hbm) for i in...  9.98 us
    ppermute x1, starting transfers between devices, shards(): peer = lax.ppermute(got, 'rep', swap)  3.37 us
  transfers between devices with their start and end apart: 2, of which 1 were waited for; matrix products, arithmetic and copies ran while one was open for 0% of the time, Pallas kernels for 4%

profile of v3, /device:TPU:1, one launch (start us, length us, event | category | flops | bytes accessed | tf_op | source)
XLA Modules:
  0.0 72.3 jit_solution(17960797289095092415)
XLA Ops:
  0.6 3.0 %route.1 = (bf16[256,1664]{1,0:T(8,128)(2,1)S(1)}, s32[8,128]{1,0:T(8,128)S(1)}) custom-call(s32[8,128]{1,0:T(8,128)} %bitcast.11, s32[8,128]{1,0:T(8,128)} %bitcast.12, s32[512,128]{1,0:T(8,128)} %bitcast.10, bf16[128,768]{1,0:T(8,128)(2,1)} %refs_3_.1), custom_call_target="tpu_custom_call" | custom-call | tf_op jit(solution)/shard_map/route/pallas_call | solution.py:245
  3.6 0.3 reshape.20
  4.0 0.0 copy-start
  4.0 41.1 %all_to_all.10 = bf16[128,2,1664]{2,1,0:T(2,128)(2,1)S(1)} all-to-all(bf16[128,2,1664]{2,1,0:T(2,128)(2,1)S(1)} %reshape.20), channel_id=1, replica_groups=mesh['grp'=128,'rep'=2] {'grp'}, dimensions={0} | all-to-all | bytes 1703936 | tf_op jit(solution)/shard_map/all_to_all | solution.py:278
  45.1 0.3 reshape.21.got_ref.refs_5_
  45.5 3.4 %collective-permute-start = (bf16[256,1664]{1,0:T(8,128)(2,1)S(1)}, bf16[256,1664]{1,0:T(8,128)(2,1)S(1)}, u32[]{:S(2)}, u32[]{:S(2)}) collective-permute-start(bf16[256,1664]{1,0:T(8,128)(2,1)S(1)} %reshape.21.got_ref.refs_5_), channel_id=1, source_target_pairs={{0,1},{1,0},{2,3},{3,2},{4,5},{5,4},{6,7},{7,6},{8,9},{9,8},{10,11... | collective-permute-start | bytes 2555912 | tf_op jit(solution)/shard_map/ppermute | solution.py:281
  48.8 0.0 copy-done
  48.8 1.9 %own_shares.1 = (bf16[512,512]{1,0:T(8,128)(2,1)S(1)}, f32[8,512]{1,0:T(8,128)S(1)}) custom-call(bf16[256,1664]{1,0:T(8,128)(2,1)S(1)} %reshape.21.got_ref.refs_5_, f32[512,768]{1,0:T(8,128)S(1)} %copy-done), custom_call_target="tpu_custom_call" | custom-call | tf_op jit(solution)/shard_map/own_shares/pallas_call | solution.py:245
  50.7 0.1 collective-permute-start.1
  50.8 1.0 %own_sums.1 = (f32[512,768]{1,0:T(8,128)S(1)}, f32[512,128]{1,0:T(8,128)S(1)}) custom-call(bf16[256,1664]{1,0:T(8,128)(2,1)S(1)} %reshape.21.got_ref.refs_5_, f32[8,512]{1,0:T(8,128)S(1)} %get-tuple-element.11.rows_ref), custom_call_target="tpu_custom_call" | custom-call | tf_op jit(solution)/shard_map/own_sums/pallas_call | solution.py:245
  51.8 0.1 collective-permute-done.1.refs_4_
  52.0 0.0 collective-permute-done.refs_3_
  52.0 3.2 %refine.1 = (f32[512,768]{1,0:T(8,128)}, f32[128,128]{1,0:T(8,128)S(1)}) custom-call(f32[512,768]{1,0:T(8,128)S(1)} %get-tuple-element.12.refs_0_, f32[512,128]{1,0:T(8,128)S(1)} %get-tuple-element.13.refs_1_, bf16[512,512]{1,0:T(8,128)(2,1)S(1)} %get-tuple-element.14.refs_2_, bf16[256,1664]{1,0:T(8,128)(2,1)S(1)} %collective-permute-done.refs_3_, ...), custom_call_target="tpu_custom_call" | custom-call | tf_op jit(solution)/shard_map/refine/pallas_call | solution.py:245
  55.2 16.3 %all_to_all.11 = f32[128,1,128]{2,1,0:T(1,128)S(1)} all-to-all(f32[128,1,128]{2,1,0:T(1,128)S(1)} %bitcast.9), channel_id=1, replica_groups=mesh['grp'=128,'rep'=2] {'grp'}, dimensions={0} | all-to-all | bytes 131072 | tf_op jit(solution)/shard_map/all_to_all | solution.py:311
  71.5 0.9 %pick.1 = f32[8,128]{1,0:T(8,128)} custom-call(f32[128,128]{1,0:T(8,128)S(1)} %bitcast.8, s32[8,128]{1,0:T(8,128)S(1)} %get-tuple-element.17.refs_1_), custom_call_target="tpu_custom_call" | custom-call | tf_op jit(solution)/shard_map/pick/pallas_call | solution.py:245
Async XLA Ops:
  4.0 44.9 %copy-start = (f32[512,768]{1,0:T(8,128)S(1)}, f32[512,768]{1,0:T(8,128)}, u32[]{:S(2)}) copy-start(f32[512,768]{1,0:T(8,128)} %refs_6_.1) | copy-start | bytes 4718596
  45.5 6.5 %collective-permute-start = (bf16[256,1664]{1,0:T(8,128)(2,1)S(1)}, bf16[256,1664]{1,0:T(8,128)(2,1)S(1)}, u32[]{:S(2)}, u32[]{:S(2)}) collective-permute-start(bf16[256,1664]{1,0:T(8,128)(2,1)S(1)} %reshape.21.got_ref.refs_5_), channel_id=1, source_target_pairs={{0,1},{1,0},{2,3},{3,2},{4,5},{5,4},{6,7},{7,6},{8,9},{9,8},{10,11... | collective-permute-start | bytes 2555912 | tf_op jit(solution)/shard_map/ppermute | solution.py:281
  50.7 1.3 %collective-permute-start.1 = (f32[8,512]{1,0:T(8,128)S(1)}, f32[8,512]{1,0:T(8,128)S(1)}, u32[]{:S(2)}, u32[]{:S(2)}) collective-permute-start(f32[8,512]{1,0:T(8,128)S(1)} %get-tuple-element.11.rows_ref), channel_id=1, source_target_pairs={{0,1},{1,0},{2,3},{3,2},{4,5},{5,4},{6,7},{7,6},{8,9},{9,8},{10,11... | collective-permute-start | bytes 49160 | tf_op jit(solution)/shard_map/ppermute | solution.py:289

commit v4 on v3

--- a/solution.py
+++ b/solution.py
@@ -33,6 +33,10 @@
         result.append(part)
         value = value - part.astype(F32)
     return result
+
+
+def dot_of_pieces(a, parts):
+    return dot(jnp.concatenate([a] * len(parts), axis=1), jnp.concatenate(parts, axis=0))
 
 
 def each(count, fn, axis):
@@ -99,26 +103,23 @@
     seat = jnp.where(live, (rank % 2) * sent + owner * half + rank // 2, -1)
     seat_ref[...] = seat
 
-    seat_iota = iota((2 * sent, rows), 0)
-    taken = jnp.zeros((2 * sent, rows), F32)
-    codes = jnp.zeros((2 * sent, rows), jnp.int32)
-    for k in range(slots):
-        match = seat_iota == seat[k : k + 1]
-        taken = jnp.where(match, 1.0, taken)
-        codes = jnp.where(match, code[k : k + 1], codes)
     copies[3].wait()
     vectors = vectors_ref[...]
-    taken = taken.astype(BF16)
-    first = (codes >> 6).astype(F32).astype(BF16)
-    second = (codes & 63).astype(F32).astype(BF16)
-    for b in range(2):
-        send_ref[:, b * feature_dim : (b + 1) * feature_dim] = dot(
-            taken[b * sent : (b + 1) * sent], vectors
-        ).astype(BF16)
-    meta = jnp.concatenate([first[:sent], second[:sent], first[sent:], second[sent:]], axis=1)
     columns = send_ref.shape[1] - 2 * feature_dim
     spread = ones_where(iota((4 * rows, columns), 0) // rows == iota((4 * rows, columns), 1))
-    send_ref[:, 2 * feature_dim :] = dot(meta, spread).astype(BF16)
+    for at in range(0, sent, rows):
+        here = slice(at, at + rows)
+        digits = []
+        for b in range(2):
+            seat_iota = iota((rows, rows), 0) + (b * sent + at)
+            codes = jnp.zeros((rows, rows), jnp.int32)
+            for k in range(slots):
+                codes = jnp.where(seat_iota == seat[k : k + 1], code[k : k + 1], codes)
+            digits += [(codes >> 6).astype(F32).astype(BF16), (codes & 63).astype(F32).astype(BF16)]
+            send_ref[here, b * feature_dim : (b + 1) * feature_dim] = dot(
+                ones_where(codes > 0), vectors
+            ).astype(BF16)
+        send_ref[here, 2 * feature_dim :] = dot(jnp.concatenate(digits, axis=1), spread).astype(BF16)
 
 
 def seat_vectors(got_ref, feature_dim, chunk):
@@ -141,11 +142,12 @@
         2, lambda b: columns[:, 2 * b : 2 * b + 1] * 64 + columns[:, 2 * b + 1 : 2 * b + 2], 0
     ).astype(jnp.int32)
     seats = code.shape[0]
-    chosen = ones_where(iota((seats, lists_here), 1) == (code >> 3))
-    chosen_ref[...] = chosen
+    for at in range(0, seats, LANES):
+        here = slice(at, at + LANES)
+        chosen_ref[here] = ones_where(iota((LANES, lists_here), 1) == (code[here] >> 3))
     total = jnp.zeros((seats, LANES), F32)
     for chunk in chunks_of(feature_dim):
-        centre = sum(dot(chosen, part) for part in pieces(centroids_ref[:, chunk], 2))
+        centre = dot_of_pieces(chosen_ref[...], pieces(centroids_ref[:, chunk], 2))
         total = total + folded((seat_vectors(got_ref, feature_dim, chunk).astype(F32) - centre) ** 2)
     sq_norms = jnp.sum(total, axis=1, keepdims=True)
     shares = (code & 7).astype(F32) / (1.0 + sq_norms / feature_dim)
@@ -166,7 +168,7 @@
     named = iota((lists_here, rows.shape[1]), 0) == rows[2:3].astype(jnp.int32)
     parts = [jnp.where(named, rows[i : i + 1], 0.0) for i in range(2)]
     totals = jnp.sum(parts[0] + parts[1], axis=1, keepdims=True)
-    return [part.astype(BF16) for part in parts], totals
+    return jnp.concatenate([part.astype(BF16) for part in parts], axis=1), totals
 
 
 def own_sums_kernel(got_ref, rows_ref, sums_ref, totals_ref):
@@ -175,12 +177,12 @@
     totals_ref[...] = jnp.broadcast_to(totals, totals_ref.shape)
     for chunk in chunks_of(feature_dim):
         vectors = seat_vectors(got_ref, feature_dim, chunk)
-        sums_ref[:, chunk] = sum(dot(part, vectors) for part in parts)
+        sums_ref[:, chunk] = dot(parts, jnp.concatenate([vectors] * 2, axis=0))
 
 
 def refine_kernel(
     sums_ref, totals_ref, chosen_ref, peer_ref, peer_rows_ref, got_ref, centroids_ref, refined_hbm,
-    dist_ref, refined_ref, sem, *, cap,
+    dist_ref, refined_ref, seat_dist_ref, sem, *, cap,
 ):
     lists_here, feature_dim = centroids_ref.shape
     parts, peer_totals = placed(peer_rows_ref, lists_here)
@@ -188,23 +190,26 @@
     chunks = chunks_of(feature_dim)
     for chunk in chunks:
         vectors = seat_vectors(peer_ref, feature_dim, chunk)
-        sums = sums_ref[:, chunk] + sum(dot(part, vectors) for part in parts)
+        sums = sums_ref[:, chunk] + dot(parts, jnp.concatenate([vectors] * 2, axis=0))
         refined_ref[:, chunk] = (centroids_ref[:, chunk] + sums) * scale
     copy = pltpu.make_async_copy(refined_ref, refined_hbm, sem)
     copy.start()
-    chosen = chosen_ref[...]
     half = cap // 2
     sent = got_ref.shape[0]
     owners = sent // half
     total = jnp.zeros((2 * sent, LANES), F32)
     for chunk in chunks:
-        centre = sum(dot(chosen, part) for part in pieces(refined_ref[:, chunk], 2))
+        centre = dot_of_pieces(chosen_ref[...], pieces(refined_ref[:, chunk], 2))
         total = total + folded((seat_vectors(got_ref, feature_dim, chunk).astype(F32) - centre) ** 2)
     dist = jnp.sum(total, axis=1, keepdims=True) / feature_dim
-    seat, lane = iota((2 * sent, LANES), 0), iota((2 * sent, LANES), 1)
-    spread = jnp.where((seat % half) * 2 + seat // sent == lane, dist, 0.0)
-    gather = ones_where((iota((owners, 2 * sent), 1) % sent) // half == iota((owners, 2 * sent), 0))
-    dist_ref[...] = sum(dot(gather, part) for part in pieces(spread, 3))
+    seat_dist_ref[...] = jnp.broadcast_to(dist, seat_dist_ref.shape)
+    lane = iota((owners, LANES), 1)
+    by_owner = jnp.zeros((owners, LANES), F32)
+    for a in range(half):
+        for b in range(2):
+            mine = seat_dist_ref[pl.ds(b * sent + a, owners, stride=half), :]
+            by_owner = jnp.where(lane == 2 * a + b, mine, by_owner)
+    dist_ref[...] = by_owner
     copy.wait()
 
 
@@ -306,7 +311,11 @@
         old_centroids,
         name="refine",
         out_hbm=(0,),
-        scratch=[pltpu.VMEM((lists_here, feature_dim), F32), pltpu.SemaphoreType.DMA],
+        scratch=[
+            pltpu.VMEM((lists_here, feature_dim), F32),
+            pltpu.VMEM((2 * sent, LANES), F32),
+            pltpu.SemaphoreType.DMA,
+        ],
     )
     seat_dist = lax.all_to_all(owner_dist.reshape(owners, 1, LANES), "grp", 0, 0, tiled=True)
     (new_dist,) = on_chip(

time: 72.5 us -> 72 us (level)
  no operation moved by 1% of the time
where the time goes in v4:
time: 72 us; the launch traced here: 71.8 us
  blocking collectives  57.4 us (80%)
  Pallas kernels  9.45 us (13%)
  starting transfers between devices  3.46 us (5%)
    all_to_all x1, blocking collectives, shards(): lax.all_to_all(send.reshape(owners, half, width), 'grp', 0, 0, tiled=True)  41.1 us
    all_to_all x1, blocking collectives, shards(): lax.all_to_all(owner_dist.reshape(owners, 1, LANES), 'grp', 0, 0, tiled=T...  16.3 us
    pallas_call x5, Pallas kernels, on_chip(): pl.pallas_call(kernel, out_shape=outs, in_specs=[spec(i, in_hbm) for i in...  9.45 us
    ppermute x1, starting transfers between devices, shards(): peer = lax.ppermute(got, 'rep', swap)  3.37 us
  transfers between devices with their start and end apart: 2, of which 1 were waited for; matrix products, arithmetic and copies ran while one was open for 0% of the time, Pallas kernels for 4%

profile of v4, /device:TPU:1, one launch (start us, length us, event | category | flops | bytes accessed | tf_op | source)
XLA Modules:
  0.0 71.8 jit_solution(2811579598071353153)
XLA Ops:
  0.6 2.5 %route.1 = (bf16[256,1664]{1,0:T(8,128)(2,1)S(1)}, s32[8,128]{1,0:T(8,128)S(1)}) custom-call(s32[8,128]{1,0:T(8,128)} %bitcast.11, s32[8,128]{1,0:T(8,128)} %bitcast.12, s32[512,128]{1,0:T(8,128)} %bitcast.10, bf16[128,768]{1,0:T(8,128)(2,1)} %refs_3_.1), custom_call_target="tpu_custom_call" | custom-call | tf_op jit(solution)/shard_map/route/pallas_call | solution.py:250
  3.1 0.3 reshape.20
  3.5 0.0 copy-start
  3.5 41.1 %all_to_all.10 = bf16[128,2,1664]{2,1,0:T(2,128)(2,1)S(1)} all-to-all(bf16[128,2,1664]{2,1,0:T(2,128)(2,1)S(1)} %reshape.20), channel_id=1, replica_groups=mesh['grp'=128,'rep'=2] {'grp'}, dimensions={0} | all-to-all | bytes 1703936 | tf_op jit(solution)/shard_map/all_to_all | solution.py:283
  44.6 0.3 reshape.21.got_ref.refs_5_
  44.9 3.4 %collective-permute-start = (bf16[256,1664]{1,0:T(8,128)(2,1)S(1)}, bf16[256,1664]{1,0:T(8,128)(2,1)S(1)}, u32[]{:S(2)}, u32[]{:S(2)}) collective-permute-start(bf16[256,1664]{1,0:T(8,128)(2,1)S(1)} %reshape.21.got_ref.refs_5_), channel_id=1, source_target_pairs={{0,1},{1,0},{2,3},{3,2},{4,5},{5,4},{6,7},{7,6},{8,9},{9,8},{10,11... | collective-permute-start | bytes 2555912 | tf_op jit(solution)/shard_map/ppermute | solution.py:286
  48.3 0.0 copy-done
  48.3 1.9 %own_shares.1 = (bf16[512,512]{1,0:T(8,128)(2,1)S(1)}, f32[8,512]{1,0:T(8,128)S(1)}) custom-call(bf16[256,1664]{1,0:T(8,128)(2,1)S(1)} %reshape.21.got_ref.refs_5_, f32[512,768]{1,0:T(8,128)S(1)} %copy-done), custom_call_target="tpu_custom_call" | custom-call | tf_op jit(solution)/shard_map/own_shares/pallas_call | solution.py:250
  50.2 0.1 collective-permute-start.1
  50.3 1.0 %own_sums.1 = (f32[512,768]{1,0:T(8,128)S(1)}, f32[512,128]{1,0:T(8,128)S(1)}) custom-call(bf16[256,1664]{1,0:T(8,128)(2,1)S(1)} %reshape.21.got_ref.refs_5_, f32[8,512]{1,0:T(8,128)S(1)} %get-tuple-element.11.rows_ref), custom_call_target="tpu_custom_call" | custom-call | tf_op jit(solution)/shard_map/own_sums/pallas_call | solution.py:250
  51.3 0.2 collective-permute-done.1.refs_4_
  51.5 0.0 collective-permute-done.refs_3_
  51.5 3.2 %refine.1 = (f32[512,768]{1,0:T(8,128)}, f32[128,128]{1,0:T(8,128)S(1)}) custom-call(f32[512,768]{1,0:T(8,128)S(1)} %get-tuple-element.12.refs_0_, f32[512,128]{1,0:T(8,128)S(1)} %get-tuple-element.13.refs_1_, bf16[512,512]{1,0:T(8,128)(2,1)S(1)} %get-tuple-element.14.refs_2_, bf16[256,1664]{1,0:T(8,128)(2,1)S(1)} %collective-permute-done.refs_3_, ...), custom_call_target="tpu_custom_call" | custom-call | tf_op jit(solution)/shard_map/refine/pallas_call | solution.py:250
  54.6 16.3 %all_to_all.11 = f32[128,1,128]{2,1,0:T(1,128)S(1)} all-to-all(f32[128,1,128]{2,1,0:T(1,128)S(1)} %bitcast.9), channel_id=1, replica_groups=mesh['grp'=128,'rep'=2] {'grp'}, dimensions={0} | all-to-all | bytes 131072 | tf_op jit(solution)/shard_map/all_to_all | solution.py:320
  70.9 0.9 %pick.1 = f32[8,128]{1,0:T(8,128)} custom-call(f32[128,128]{1,0:T(8,128)S(1)} %bitcast.8, s32[8,128]{1,0:T(8,128)S(1)} %get-tuple-element.17.refs_1_), custom_call_target="tpu_custom_call" | custom-call | tf_op jit(solution)/shard_map/pick/pallas_call | solution.py:250
Async XLA Ops:
  3.5 44.9 %copy-start = (f32[512,768]{1,0:T(8,128)S(1)}, f32[512,768]{1,0:T(8,128)}, u32[]{:S(2)}) copy-start(f32[512,768]{1,0:T(8,128)} %refs_6_.1) | copy-start | bytes 4718596
  44.9 6.5 %collective-permute-start = (bf16[256,1664]{1,0:T(8,128)(2,1)S(1)}, bf16[256,1664]{1,0:T(8,128)(2,1)S(1)}, u32[]{:S(2)}, u32[]{:S(2)}) collective-permute-start(bf16[256,1664]{1,0:T(8,128)(2,1)S(1)} %reshape.21.got_ref.refs_5_), channel_id=1, source_target_pairs={{0,1},{1,0},{2,3},{3,2},{4,5},{5,4},{6,7},{7,6},{8,9},{9,8},{10,11... | collective-permute-start | bytes 2555912 | tf_op jit(solution)/shard_map/ppermute | solution.py:286
  50.2 1.3 %collective-permute-start.1 = (f32[8,512]{1,0:T(8,128)S(1)}, f32[8,512]{1,0:T(8,128)S(1)}, u32[]{:S(2)}, u32[]{:S(2)}) collective-permute-start(f32[8,512]{1,0:T(8,128)S(1)} %get-tuple-element.11.rows_ref), channel_id=1, source_target_pairs={{0,1},{1,0},{2,3},{3,2},{4,5},{5,4},{6,7},{7,6},{8,9},{9,8},{10,11... | collective-permute-start | bytes 49160 | tf_op jit(solution)/shard_map/ppermute | solution.py:294

commit v5 on v4

--- a/solution.py
+++ b/solution.py
@@ -145,22 +145,24 @@
     for at in range(0, seats, LANES):
         here = slice(at, at + LANES)
         chosen_ref[here] = ones_where(iota((LANES, lists_here), 1) == (code[here] >> 3))
+    to_rows = ones_where(iota((8, LANES), 0) == iota((8, LANES), 1))
+    digits = dot(to_rows, meta, (1, 1))
+    code_row = each(
+        2, lambda b: digits[2 * b : 2 * b + 1] * 64 + digits[2 * b + 1 : 2 * b + 2], 1
+    ).astype(jnp.int32)
     total = jnp.zeros((seats, LANES), F32)
     for chunk in chunks_of(feature_dim):
         centre = dot_of_pieces(chosen_ref[...], pieces(centroids_ref[:, chunk], 2))
         total = total + folded((seat_vectors(got_ref, feature_dim, chunk).astype(F32) - centre) ** 2)
-    sq_norms = jnp.sum(total, axis=1, keepdims=True)
-    shares = (code & 7).astype(F32) / (1.0 + sq_norms / feature_dim)
+    sq_norms = dot(jnp.ones((8, 3 * LANES), BF16), jnp.concatenate(pieces(total, 3), axis=1), (1, 1))
+    shares = (code_row % 8).astype(F32) / (1.0 + sq_norms[0:1] / feature_dim)
     high, low = pieces(shares, 2)
-    lists = code >> 3
-    lane = iota((seats, LANES), 1)
-    block = jnp.where(lane == 0, high.astype(F32), jnp.where(lane == 1, low.astype(F32), 0.0))
-    block = jnp.where(lane == 2, (lists >> 8).astype(F32), block)
-    block = jnp.where(lane == 3, (lists & 255).astype(F32), block)
-    to_rows = ones_where(iota((8, LANES), 0) == iota((8, LANES), 1))
-    rows = dot(to_rows, block.astype(BF16), (1, 1))
     row = iota((8, seats), 0)
-    rows_ref[...] = jnp.where(row == 2, rows[2:3] * 256 + rows[3:4], rows)
+    rows_ref[...] = jnp.where(
+        row == 0,
+        high.astype(F32),
+        jnp.where(row == 1, low.astype(F32), (code_row >> 3).astype(F32)),
+    )
 
 
 def placed(rows_ref, lists_here):

time: 72 us -> 71.7 us (level)
  no operation moved by 1% of the time
where the time goes in v5:
time: 71.7 us; the launch traced here: 71.5 us
  blocking collectives  57.4 us (80%)
  Pallas kernels  9.13 us (13%)
  starting transfers between devices  3.48 us (5%)
    all_to_all x1, blocking collectives, shards(): lax.all_to_all(send.reshape(owners, half, width), 'grp', 0, 0, tiled=True)  41.1 us
    all_to_all x1, blocking collectives, shards(): lax.all_to_all(owner_dist.reshape(owners, 1, LANES), 'grp', 0, 0, tiled=T...  16.3 us
    pallas_call x5, Pallas kernels, on_chip(): pl.pallas_call(kernel, out_shape=outs, in_specs=[spec(i, in_hbm) for i in...  9.13 us
    ppermute x1, starting transfers between devices, shards(): peer = lax.ppermute(got, 'rep', swap)  3.37 us
  transfers between devices with their start and end apart: 2, of which 1 were waited for; matrix products, arithmetic and copies ran while one was open for 0% of the time, Pallas kernels for 4%

profile of v5, /device:TPU:1, one launch (start us, length us, event | category | flops | bytes accessed | tf_op | source)
XLA Modules:
  0.0 71.5 jit_solution(17841020035422630893)
XLA Ops:
  0.6 2.5 %route.1 = (bf16[256,1664]{1,0:T(8,128)(2,1)S(1)}, s32[8,128]{1,0:T(8,128)S(1)}) custom-call(s32[8,128]{1,0:T(8,128)} %bitcast.11, s32[8,128]{1,0:T(8,128)} %bitcast.12, s32[512,128]{1,0:T(8,128)} %bitcast.10, bf16[128,768]{1,0:T(8,128)(2,1)} %refs_3_.1), custom_call_target="tpu_custom_call" | custom-call | tf_op jit(solution)/shard_map/route/pallas_call | solution.py:252
  3.1 0.3 reshape.20
  3.5 0.0 copy-start
  3.5 41.1 %all_to_all.10 = bf16[128,2,1664]{2,1,0:T(2,128)(2,1)S(1)} all-to-all(bf16[128,2,1664]{2,1,0:T(2,128)(2,1)S(1)} %reshape.20), channel_id=1, replica_groups=mesh['grp'=128,'rep'=2] {'grp'}, dimensions={0} | all-to-all | bytes 1703936 | tf_op jit(solution)/shard_map/all_to_all | solution.py:285
  44.6 0.3 reshape.21.got_ref.refs_5_
  44.9 3.4 %collective-permute-start = (bf16[256,1664]{1,0:T(8,128)(2,1)S(1)}, bf16[256,1664]{1,0:T(8,128)(2,1)S(1)}, u32[]{:S(2)}, u32[]{:S(2)}) collective-permute-start(bf16[256,1664]{1,0:T(8,128)(2,1)S(1)} %reshape.21.got_ref.refs_5_), channel_id=1, source_target_pairs={{0,1},{1,0},{2,3},{3,2},{4,5},{5,4},{6,7},{7,6},{8,9},{9,8},{10,11... | collective-permute-start | bytes 2555912 | tf_op jit(solution)/shard_map/ppermute | solution.py:288
  48.3 0.0 copy-done
  48.3 1.6 %own_shares.1 = (bf16[512,512]{1,0:T(8,128)(2,1)S(1)}, f32[8,512]{1,0:T(8,128)S(1)}) custom-call(bf16[256,1664]{1,0:T(8,128)(2,1)S(1)} %reshape.21.got_ref.refs_5_, f32[512,768]{1,0:T(8,128)S(1)} %copy-done), custom_call_target="tpu_custom_call" | custom-call | tf_op jit(solution)/shard_map/own_shares/pallas_call | solution.py:252
  49.9 0.1 collective-permute-start.1
  50.0 1.0 %own_sums.1 = (f32[512,768]{1,0:T(8,128)S(1)}, f32[512,128]{1,0:T(8,128)S(1)}) custom-call(bf16[256,1664]{1,0:T(8,128)(2,1)S(1)} %reshape.21.got_ref.refs_5_, f32[8,512]{1,0:T(8,128)S(1)} %get-tuple-element.11.rows_ref), custom_call_target="tpu_custom_call" | custom-call | tf_op jit(solution)/shard_map/own_sums/pallas_call | solution.py:252
  51.0 0.2 collective-permute-done.1.refs_4_
  51.2 0.0 collective-permute-done.refs_3_
  51.2 3.2 %refine.1 = (f32[512,768]{1,0:T(8,128)}, f32[128,128]{1,0:T(8,128)S(1)}) custom-call(f32[512,768]{1,0:T(8,128)S(1)} %get-tuple-element.12.refs_0_, f32[512,128]{1,0:T(8,128)S(1)} %get-tuple-element.13.refs_1_, bf16[512,512]{1,0:T(8,128)(2,1)S(1)} %get-tuple-element.14.refs_2_, bf16[256,1664]{1,0:T(8,128)(2,1)S(1)} %collective-permute-done.refs_3_, ...), custom_call_target="tpu_custom_call" | custom-call | tf_op jit(solution)/shard_map/refine/pallas_call | solution.py:252
  54.3 16.3 %all_to_all.11 = f32[128,1,128]{2,1,0:T(1,128)S(1)} all-to-all(f32[128,1,128]{2,1,0:T(1,128)S(1)} %bitcast.9), channel_id=1, replica_groups=mesh['grp'=128,'rep'=2] {'grp'}, dimensions={0} | all-to-all | bytes 131072 | tf_op jit(solution)/shard_map/all_to_all | solution.py:322
  70.6 0.9 %pick.1 = f32[8,128]{1,0:T(8,128)} custom-call(f32[128,128]{1,0:T(8,128)S(1)} %bitcast.8, s32[8,128]{1,0:T(8,128)S(1)} %get-tuple-element.17.refs_1_), custom_call_target="tpu_custom_call" | custom-call | tf_op jit(solution)/shard_map/pick/pallas_call | solution.py:252
Async XLA Ops:
  3.5 44.9 %copy-start = (f32[512,768]{1,0:T(8,128)S(1)}, f32[512,768]{1,0:T(8,128)}, u32[]{:S(2)}) copy-start(f32[512,768]{1,0:T(8,128)} %refs_6_.1) | copy-start | bytes 4718596
  44.9 6.2 %collective-permute-start = (bf16[256,1664]{1,0:T(8,128)(2,1)S(1)}, bf16[256,1664]{1,0:T(8,128)(2,1)S(1)}, u32[]{:S(2)}, u32[]{:S(2)}) collective-permute-start(bf16[256,1664]{1,0:T(8,128)(2,1)S(1)} %reshape.21.got_ref.refs_5_), channel_id=1, source_target_pairs={{0,1},{1,0},{2,3},{3,2},{4,5},{5,4},{6,7},{7,6},{8,9},{9,8},{10,11... | collective-permute-start | bytes 2555912 | tf_op jit(solution)/shard_map/ppermute | solution.py:288
  49.9 1.3 %collective-permute-start.1 = (f32[8,512]{1,0:T(8,128)S(1)}, f32[8,512]{1,0:T(8,128)S(1)}, u32[]{:S(2)}, u32[]{:S(2)}) collective-permute-start(f32[8,512]{1,0:T(8,128)S(1)} %get-tuple-element.11.rows_ref), channel_id=1, source_target_pairs={{0,1},{1,0},{2,3},{3,2},{4,5},{5,4},{6,7},{7,6},{8,9},{9,8},{10,11... | collective-permute-start | bytes 49160 | tf_op jit(solution)/shard_map/ppermute | solution.py:296

commit v6 on v5

--- a/solution.py
+++ b/solution.py
@@ -7,6 +7,7 @@
 
 LANES = 128
 CHUNK = 256
+BLOCKS = 2
 VMEM_LIMIT = 24 * 2**20
 F32 = jnp.float32
 BF16 = jnp.bfloat16
@@ -184,18 +185,24 @@
 
 def refine_kernel(
     sums_ref, totals_ref, chosen_ref, peer_ref, peer_rows_ref, got_ref, centroids_ref, refined_hbm,
-    dist_ref, refined_ref, seat_dist_ref, sem, *, cap,
+    dist_ref, refined_ref, seat_dist_ref, sems, *, cap,
 ):
     lists_here, feature_dim = centroids_ref.shape
     parts, peer_totals = placed(peer_rows_ref, lists_here)
     scale = 1.0 / (1.0 + (totals_ref[:, 0:1] + peer_totals))
     chunks = chunks_of(feature_dim)
-    for chunk in chunks:
-        vectors = seat_vectors(peer_ref, feature_dim, chunk)
-        sums = sums_ref[:, chunk] + dot(parts, jnp.concatenate([vectors] * 2, axis=0))
-        refined_ref[:, chunk] = (centroids_ref[:, chunk] + sums) * scale
-    copy = pltpu.make_async_copy(refined_ref, refined_hbm, sem)
-    copy.start()
+    step = lists_here // BLOCKS
+    copies = []
+    for i in range(BLOCKS):
+        here = slice(i * step, (i + 1) * step)
+        for chunk in chunks:
+            vectors = seat_vectors(peer_ref, feature_dim, chunk)
+            sums = sums_ref[here, chunk] + dot(parts[here], jnp.concatenate([vectors] * 2, axis=0))
+            refined_ref[here, chunk] = (centroids_ref[here, chunk] + sums) * scale[here]
+        copies.append(
+            pltpu.make_async_copy(refined_ref.at[here], refined_hbm.at[here], sems.at[i])
+        )
+        copies[-1].start()
     half = cap // 2
     sent = got_ref.shape[0]
     owners = sent // half
@@ -212,7 +219,8 @@
             mine = seat_dist_ref[pl.ds(b * sent + a, owners, stride=half), :]
             by_owner = jnp.where(lane == 2 * a + b, mine, by_owner)
     dist_ref[...] = by_owner
-    copy.wait()
+    for copy in copies:
+        copy.wait()
 
 
 def pick_kernel(dist_ref, seat_ref, out_ref, *, cap):
@@ -316,7 +324,7 @@
         scratch=[
             pltpu.VMEM((lists_here, feature_dim), F32),
             pltpu.VMEM((2 * sent, LANES), F32),
-            pltpu.SemaphoreType.DMA,
+            pltpu.SemaphoreType.DMA((BLOCKS,)),
         ],
     )
     seat_dist = lax.all_to_all(owner_dist.reshape(owners, 1, LANES), "grp", 0, 0, tiled=True)

time: 71.7 us -> 70.7 us (0.986)
  Pallas kernels: 9.13 us -> 8.16 us
    pallas_call x5, Pallas kernels: 9.13 us -> 8.16 us  [on_chip(): pl.pallas_call(kernel, out_shape=outs, in_specs=[spec(i, in_hbm) for i in...]
where the time goes in v6:
time: 70.7 us; the launch traced here: 70.6 us
  blocking collectives  57.4 us (81%)
  Pallas kernels  8.16 us (12%)
  starting transfers between devices  3.48 us (5%)
    all_to_all x1, blocking collectives, shards(): lax.all_to_all(send.reshape(owners, half, width), 'grp', 0, 0, tiled=True)  41.1 us
    all_to_all x1, blocking collectives, shards(): lax.all_to_all(owner_dist.reshape(owners, 1, LANES), 'grp', 0, 0, tiled=T...  16.3 us
    pallas_call x5, Pallas kernels, on_chip(): pl.pallas_call(kernel, out_shape=outs, in_specs=[spec(i, in_hbm) for i in...  8.16 us
    ppermute x1, starting transfers between devices, shards(): peer = lax.ppermute(got, 'rep', swap)  3.37 us
  transfers between devices with their start and end apart: 2, of which 1 were waited for; matrix products, arithmetic and copies ran while one was open for 0% of the time, Pallas kernels for 4%

profile of v6, /device:TPU:1, one launch (start us, length us, event | category | flops | bytes accessed | tf_op | source)
XLA Modules:
  0.0 70.6 jit_solution(8623353642077624123)
XLA Ops:
  0.6 2.5 %route.1 = (bf16[256,1664]{1,0:T(8,128)(2,1)S(1)}, s32[8,128]{1,0:T(8,128)S(1)}) custom-call(s32[8,128]{1,0:T(8,128)} %bitcast.11, s32[8,128]{1,0:T(8,128)} %bitcast.12, s32[512,128]{1,0:T(8,128)} %bitcast.10, bf16[128,768]{1,0:T(8,128)(2,1)} %refs_3_.1), custom_call_target="tpu_custom_call" | custom-call | tf_op jit(solution)/shard_map/route/pallas_call | solution.py:260
  3.1 0.3 reshape.20
  3.5 0.0 copy-start
  3.5 41.1 %all_to_all.10 = bf16[128,2,1664]{2,1,0:T(2,128)(2,1)S(1)} all-to-all(bf16[128,2,1664]{2,1,0:T(2,128)(2,1)S(1)} %reshape.20), channel_id=1, replica_groups=mesh['grp'=128,'rep'=2] {'grp'}, dimensions={0} | all-to-all | bytes 1703936 | tf_op jit(solution)/shard_map/all_to_all | solution.py:293
  44.6 0.3 reshape.21.got_ref.refs_5_
  44.9 3.4 %collective-permute-start = (bf16[256,1664]{1,0:T(8,128)(2,1)S(1)}, bf16[256,1664]{1,0:T(8,128)(2,1)S(1)}, u32[]{:S(2)}, u32[]{:S(2)}) collective-permute-start(bf16[256,1664]{1,0:T(8,128)(2,1)S(1)} %reshape.21.got_ref.refs_5_), channel_id=1, source_target_pairs={{0,1},{1,0},{2,3},{3,2},{4,5},{5,4},{6,7},{7,6},{8,9},{9,8},{10,11... | collective-permute-start | bytes 2555912 | tf_op jit(solution)/shard_map/ppermute | solution.py:296
  48.3 0.0 copy-done
  48.3 1.6 %own_shares.1 = (bf16[512,512]{1,0:T(8,128)(2,1)S(1)}, f32[8,512]{1,0:T(8,128)S(1)}) custom-call(bf16[256,1664]{1,0:T(8,128)(2,1)S(1)} %reshape.21.got_ref.refs_5_, f32[512,768]{1,0:T(8,128)S(1)} %copy-done), custom_call_target="tpu_custom_call" | custom-call | tf_op jit(solution)/shard_map/own_shares/pallas_call | solution.py:260
  49.9 0.1 collective-permute-start.1
  50.0 1.0 %own_sums.1 = (f32[512,768]{1,0:T(8,128)S(1)}, f32[512,128]{1,0:T(8,128)S(1)}) custom-call(bf16[256,1664]{1,0:T(8,128)(2,1)S(1)} %reshape.21.got_ref.refs_5_, f32[8,512]{1,0:T(8,128)S(1)} %get-tuple-element.11.rows_ref), custom_call_target="tpu_custom_call" | custom-call | tf_op jit(solution)/shard_map/own_sums/pallas_call | solution.py:260
  51.0 0.2 collective-permute-done.1.refs_4_
  51.2 0.0 collective-permute-done.refs_3_
  51.2 2.2 %refine.1 = (f32[512,768]{1,0:T(8,128)}, f32[128,128]{1,0:T(8,128)S(1)}) custom-call(f32[512,768]{1,0:T(8,128)S(1)} %get-tuple-element.12.refs_0_, f32[512,128]{1,0:T(8,128)S(1)} %get-tuple-element.13.refs_1_, bf16[512,512]{1,0:T(8,128)(2,1)S(1)} %get-tuple-element.14.refs_2_, bf16[256,1664]{1,0:T(8,128)(2,1)S(1)} %collective-permute-done.refs_3_, ...), custom_call_target="tpu_custom_call" | custom-call | tf_op jit(solution)/shard_map/refine/pallas_call | solution.py:260
  53.4 16.3 %all_to_all.11 = f32[128,1,128]{2,1,0:T(1,128)S(1)} all-to-all(f32[128,1,128]{2,1,0:T(1,128)S(1)} %bitcast.9), channel_id=1, replica_groups=mesh['grp'=128,'rep'=2] {'grp'}, dimensions={0} | all-to-all | bytes 131072 | tf_op jit(solution)/shard_map/all_to_all | solution.py:330
  69.7 0.9 %pick.1 = f32[8,128]{1,0:T(8,128)} custom-call(f32[128,128]{1,0:T(8,128)S(1)} %bitcast.8, s32[8,128]{1,0:T(8,128)S(1)} %get-tuple-element.17.refs_1_), custom_call_target="tpu_custom_call" | custom-call | tf_op jit(solution)/shard_map/pick/pallas_call | solution.py:260
Async XLA Ops:
  3.5 44.9 %copy-start = (f32[512,768]{1,0:T(8,128)S(1)}, f32[512,768]{1,0:T(8,128)}, u32[]{:S(2)}) copy-start(f32[512,768]{1,0:T(8,128)} %refs_6_.1) | copy-start | bytes 4718596
  44.9 6.2 %collective-permute-start = (bf16[256,1664]{1,0:T(8,128)(2,1)S(1)}, bf16[256,1664]{1,0:T(8,128)(2,1)S(1)}, u32[]{:S(2)}, u32[]{:S(2)}) collective-permute-start(bf16[256,1664]{1,0:T(8,128)(2,1)S(1)} %reshape.21.got_ref.refs_5_), channel_id=1, source_target_pairs={{0,1},{1,0},{2,3},{3,2},{4,5},{5,4},{6,7},{7,6},{8,9},{9,8},{10,11... | collective-permute-start | bytes 2555912 | tf_op jit(solution)/shard_map/ppermute | solution.py:296
  49.9 1.3 %collective-permute-start.1 = (f32[8,512]{1,0:T(8,128)S(1)}, f32[8,512]{1,0:T(8,128)S(1)}, u32[]{:S(2)}, u32[]{:S(2)}) collective-permute-start(f32[8,512]{1,0:T(8,128)S(1)} %get-tuple-element.11.rows_ref), channel_id=1, source_target_pairs={{0,1},{1,0},{2,3},{3,2},{4,5},{5,4},{6,7},{7,6},{8,9},{9,8},{10,11... | collective-permute-start | bytes 49160 | tf_op jit(solution)/shard_map/ppermute | solution.py:304

commit v7 on v6

--- a/solution.py
+++ b/solution.py
@@ -234,7 +234,8 @@
     by_rank = dist_ref[...].T[:8]
     owner_iota = iota((owners, rows), 0)
     at_owner = each(slots, lambda k: ones_where(owner_iota == owner[k : k + 1]), 1)
-    found = sum(dot(part, at_owner) for part in pieces(by_rank, 3))
+    found = dot(jnp.concatenate(pieces(by_rank, 3), axis=0), at_owner)
+    found = found[:8] + found[8:16] + found[16:]
     rank_iota = iota((8, rows), 0)
     picked = each(
         slots,

time: 70.7 us -> 70.7 us (level)
  no operation moved by 1% of the time
where the time goes in v7:
time: 70.7 us; the launch traced here: 70.5 us
  blocking collectives  57.4 us (81%)
  Pallas kernels  8.1 us (11%)
  starting transfers between devices  3.48 us (5%)
    all_to_all x1, blocking collectives, shards(): lax.all_to_all(send.reshape(owners, half, width), 'grp', 0, 0, tiled=True)  41.1 us
    all_to_all x1, blocking collectives, shards(): lax.all_to_all(owner_dist.reshape(owners, 1, LANES), 'grp', 0, 0, tiled=T...  16.3 us
    pallas_call x5, Pallas kernels, on_chip(): pl.pallas_call(kernel, out_shape=outs, in_specs=[spec(i, in_hbm) for i in...  8.1 us
    ppermute x1, starting transfers between devices, shards(): peer = lax.ppermute(got, 'rep', swap)  3.37 us
  transfers between devices with their start and end apart: 2, of which 1 were waited for; matrix products, arithmetic and copies ran while one was open for 0% of the time, Pallas kernels for 4%

profile of v7, /device:TPU:1, one launch (start us, length us, event | category | flops | bytes accessed | tf_op | source)
XLA Modules:
  0.0 70.5 jit_solution(6666427920459832488)
XLA Ops:
  0.6 2.5 %route.1 = (bf16[256,1664]{1,0:T(8,128)(2,1)S(1)}, s32[8,128]{1,0:T(8,128)S(1)}) custom-call(s32[8,128]{1,0:T(8,128)} %bitcast.11, s32[8,128]{1,0:T(8,128)} %bitcast.12, s32[512,128]{1,0:T(8,128)} %bitcast.10, bf16[128,768]{1,0:T(8,128)(2,1)} %refs_3_.1), custom_call_target="tpu_custom_call" | custom-call | tf_op jit(solution)/shard_map/route/pallas_call | solution.py:261
  3.1 0.3 reshape.20
  3.5 0.0 copy-start
  3.5 41.1 %all_to_all.10 = bf16[128,2,1664]{2,1,0:T(2,128)(2,1)S(1)} all-to-all(bf16[128,2,1664]{2,1,0:T(2,128)(2,1)S(1)} %reshape.20), channel_id=1, replica_groups=mesh['grp'=128,'rep'=2] {'grp'}, dimensions={0} | all-to-all | bytes 1703936 | tf_op jit(solution)/shard_map/all_to_all | solution.py:294
  44.6 0.3 reshape.21.got_ref.refs_5_
  44.9 3.4 %collective-permute-start = (bf16[256,1664]{1,0:T(8,128)(2,1)S(1)}, bf16[256,1664]{1,0:T(8,128)(2,1)S(1)}, u32[]{:S(2)}, u32[]{:S(2)}) collective-permute-start(bf16[256,1664]{1,0:T(8,128)(2,1)S(1)} %reshape.21.got_ref.refs_5_), channel_id=1, source_target_pairs={{0,1},{1,0},{2,3},{3,2},{4,5},{5,4},{6,7},{7,6},{8,9},{9,8},{10,11... | collective-permute-start | bytes 2555912 | tf_op jit(solution)/shard_map/ppermute | solution.py:297
  48.3 0.0 copy-done
  48.3 1.6 %own_shares.1 = (bf16[512,512]{1,0:T(8,128)(2,1)S(1)}, f32[8,512]{1,0:T(8,128)S(1)}) custom-call(bf16[256,1664]{1,0:T(8,128)(2,1)S(1)} %reshape.21.got_ref.refs_5_, f32[512,768]{1,0:T(8,128)S(1)} %copy-done), custom_call_target="tpu_custom_call" | custom-call | tf_op jit(solution)/shard_map/own_shares/pallas_call | solution.py:261
  49.9 0.1 collective-permute-start.1
  50.0 1.0 %own_sums.1 = (f32[512,768]{1,0:T(8,128)S(1)}, f32[512,128]{1,0:T(8,128)S(1)}) custom-call(bf16[256,1664]{1,0:T(8,128)(2,1)S(1)} %reshape.21.got_ref.refs_5_, f32[8,512]{1,0:T(8,128)S(1)} %get-tuple-element.11.rows_ref), custom_call_target="tpu_custom_call" | custom-call | tf_op jit(solution)/shard_map/own_sums/pallas_call | solution.py:261
  51.0 0.2 collective-permute-done.1.refs_4_
  51.2 0.0 collective-permute-done.refs_3_
  51.2 2.2 %refine.1 = (f32[512,768]{1,0:T(8,128)}, f32[128,128]{1,0:T(8,128)S(1)}) custom-call(f32[512,768]{1,0:T(8,128)S(1)} %get-tuple-element.12.refs_0_, f32[512,128]{1,0:T(8,128)S(1)} %get-tuple-element.13.refs_1_, bf16[512,512]{1,0:T(8,128)(2,1)S(1)} %get-tuple-element.14.refs_2_, bf16[256,1664]{1,0:T(8,128)(2,1)S(1)} %collective-permute-done.refs_3_, ...), custom_call_target="tpu_custom_call" | custom-call | tf_op jit(solution)/shard_map/refine/pallas_call | solution.py:261
  53.4 16.3 %all_to_all.11 = f32[128,1,128]{2,1,0:T(1,128)S(1)} all-to-all(f32[128,1,128]{2,1,0:T(1,128)S(1)} %bitcast.9), channel_id=1, replica_groups=mesh['grp'=128,'rep'=2] {'grp'}, dimensions={0} | all-to-all | bytes 131072 | tf_op jit(solution)/shard_map/all_to_all | solution.py:331
  69.7 0.8 %pick.1 = f32[8,128]{1,0:T(8,128)} custom-call(f32[128,128]{1,0:T(8,128)S(1)} %bitcast.8, s32[8,128]{1,0:T(8,128)S(1)} %get-tuple-element.17.refs_1_), custom_call_target="tpu_custom_call" | custom-call | tf_op jit(solution)/shard_map/pick/pallas_call | solution.py:261
Async XLA Ops:
  3.5 44.9 %copy-start = (f32[512,768]{1,0:T(8,128)S(1)}, f32[512,768]{1,0:T(8,128)}, u32[]{:S(2)}) copy-start(f32[512,768]{1,0:T(8,128)} %refs_6_.1) | copy-start | bytes 4718596
  44.9 6.2 %collective-permute-start = (bf16[256,1664]{1,0:T(8,128)(2,1)S(1)}, bf16[256,1664]{1,0:T(8,128)(2,1)S(1)}, u32[]{:S(2)}, u32[]{:S(2)}) collective-permute-start(bf16[256,1664]{1,0:T(8,128)(2,1)S(1)} %reshape.21.got_ref.refs_5_), channel_id=1, source_target_pairs={{0,1},{1,0},{2,3},{3,2},{4,5},{5,4},{6,7},{7,6},{8,9},{9,8},{10,11... | collective-permute-start | bytes 2555912 | tf_op jit(solution)/shard_map/ppermute | solution.py:297
  49.9 1.3 %collective-permute-start.1 = (f32[8,512]{1,0:T(8,128)S(1)}, f32[8,512]{1,0:T(8,128)S(1)}, u32[]{:S(2)}, u32[]{:S(2)}) collective-permute-start(f32[8,512]{1,0:T(8,128)S(1)} %get-tuple-element.11.rows_ref), channel_id=1, source_target_pairs={{0,1},{1,0},{2,3},{3,2},{4,5},{5,4},{6,7},{7,6},{8,9},{9,8},{10,11... | collective-permute-start | bytes 49160 | tf_op jit(solution)/shard_map/ppermute | solution.py:305

commit v8 on v7

--- a/solution.py
+++ b/solution.py
@@ -38,6 +38,11 @@
 
 def dot_of_pieces(a, parts):
     return dot(jnp.concatenate([a] * len(parts), axis=1), jnp.concatenate(parts, axis=0))
+
+
+def sum_of_parts(parts, b):
+    both = dot(jnp.concatenate(parts, axis=0), b)
+    return both[: parts[0].shape[0]] + both[parts[0].shape[0] :]
 
 
 def each(count, fn, axis):
@@ -171,7 +176,7 @@
     named = iota((lists_here, rows.shape[1]), 0) == rows[2:3].astype(jnp.int32)
     parts = [jnp.where(named, rows[i : i + 1], 0.0) for i in range(2)]
     totals = jnp.sum(parts[0] + parts[1], axis=1, keepdims=True)
-    return jnp.concatenate([part.astype(BF16) for part in parts], axis=1), totals
+    return [part.astype(BF16) for part in parts], totals
 
 
 def own_sums_kernel(got_ref, rows_ref, sums_ref, totals_ref):
@@ -180,7 +185,7 @@
     totals_ref[...] = jnp.broadcast_to(totals, totals_ref.shape)
     for chunk in chunks_of(feature_dim):
         vectors = seat_vectors(got_ref, feature_dim, chunk)
-        sums_ref[:, chunk] = dot(parts, jnp.concatenate([vectors] * 2, axis=0))
+        sums_ref[:, chunk] = sum_of_parts(parts, vectors)
 
 
 def refine_kernel(
@@ -197,7 +202,7 @@
         here = slice(i * step, (i + 1) * step)
         for chunk in chunks:
             vectors = seat_vectors(peer_ref, feature_dim, chunk)
-            sums = sums_ref[here, chunk] + dot(parts[here], jnp.concatenate([vectors] * 2, axis=0))
+            sums = sums_ref[here, chunk] + sum_of_parts([part[here] for part in parts], vectors)
             refined_ref[here, chunk] = (centroids_ref[here, chunk] + sums) * scale[here]
         copies.append(
             pltpu.make_async_copy(refined_ref.at[here], refined_hbm.at[here], sems.at[i])

time: 70.7 us -> 70.9 us (level)
  no operation moved by 1% of the time
where the time goes in v8:
time: 70.9 us; the launch traced here: 70.7 us
  blocking collectives  57.4 us (81%)
  Pallas kernels  8.37 us (12%)
  starting transfers between devices  3.48 us (5%)
    all_to_all x1, blocking collectives, shards(): lax.all_to_all(send.reshape(owners, half, width), 'grp', 0, 0, tiled=True)  41.1 us
    all_to_all x1, blocking collectives, shards(): lax.all_to_all(owner_dist.reshape(owners, 1, LANES), 'grp', 0, 0, tiled=T...  16.3 us
    pallas_call x5, Pallas kernels, on_chip(): pl.pallas_call(kernel, out_shape=outs, in_specs=[spec(i, in_hbm) for i in...  8.37 us
    ppermute x1, starting transfers between devices, shards(): peer = lax.ppermute(got, 'rep', swap)  3.37 us
  transfers between devices with their start and end apart: 2, of which 1 were waited for; matrix products, arithmetic and copies ran while one was open for 0% of the time, Pallas kernels for 4%

profile of v8, /device:TPU:1, one launch (start us, length us, event | category | flops | bytes accessed | tf_op | source)
XLA Modules:
  0.0 70.7 jit_solution(14463747426457156633)
XLA Ops:
  0.6 2.5 %route.1 = (bf16[256,1664]{1,0:T(8,128)(2,1)S(1)}, s32[8,128]{1,0:T(8,128)S(1)}) custom-call(s32[8,128]{1,0:T(8,128)} %bitcast.11, s32[8,128]{1,0:T(8,128)} %bitcast.12, s32[512,128]{1,0:T(8,128)} %bitcast.10, bf16[128,768]{1,0:T(8,128)(2,1)} %refs_3_.1), custom_call_target="tpu_custom_call" | custom-call | tf_op jit(solution)/shard_map/route/pallas_call | solution.py:266
  3.1 0.3 reshape.20
  3.5 0.0 copy-start
  3.5 41.1 %all_to_all.10 = bf16[128,2,1664]{2,1,0:T(2,128)(2,1)S(1)} all-to-all(bf16[128,2,1664]{2,1,0:T(2,128)(2,1)S(1)} %reshape.20), channel_id=1, replica_groups=mesh['grp'=128,'rep'=2] {'grp'}, dimensions={0} | all-to-all | bytes 1703936 | tf_op jit(solution)/shard_map/all_to_all | solution.py:299
  44.6 0.3 reshape.21.got_ref.refs_5_
  44.9 3.4 %collective-permute-start = (bf16[256,1664]{1,0:T(8,128)(2,1)S(1)}, bf16[256,1664]{1,0:T(8,128)(2,1)S(1)}, u32[]{:S(2)}, u32[]{:S(2)}) collective-permute-start(bf16[256,1664]{1,0:T(8,128)(2,1)S(1)} %reshape.21.got_ref.refs_5_), channel_id=1, source_target_pairs={{0,1},{1,0},{2,3},{3,2},{4,5},{5,4},{6,7},{7,6},{8,9},{9,8},{10,11... | collective-permute-start | bytes 2555912 | tf_op jit(solution)/shard_map/ppermute | solution.py:302
  48.3 0.0 copy-done
  48.3 1.6 %own_shares.1 = (bf16[512,512]{1,0:T(8,128)(2,1)S(1)}, f32[8,512]{1,0:T(8,128)S(1)}) custom-call(bf16[256,1664]{1,0:T(8,128)(2,1)S(1)} %reshape.21.got_ref.refs_5_, f32[512,768]{1,0:T(8,128)S(1)} %copy-done), custom_call_target="tpu_custom_call" | custom-call | tf_op jit(solution)/shard_map/own_shares/pallas_call | solution.py:266
  49.9 0.1 collective-permute-start.1
  50.0 1.0 %own_sums.1 = (f32[512,768]{1,0:T(8,128)S(1)}, f32[512,128]{1,0:T(8,128)S(1)}) custom-call(bf16[256,1664]{1,0:T(8,128)(2,1)S(1)} %reshape.21.got_ref.refs_5_, f32[8,512]{1,0:T(8,128)S(1)} %get-tuple-element.11.rows_ref), custom_call_target="tpu_custom_call" | custom-call | tf_op jit(solution)/shard_map/own_sums/pallas_call | solution.py:266
  51.0 0.1 collective-permute-done.1.refs_4_
  51.2 0.0 collective-permute-done.refs_3_
  51.2 2.5 %refine.1 = (f32[512,768]{1,0:T(8,128)}, f32[128,128]{1,0:T(8,128)S(1)}) custom-call(f32[512,768]{1,0:T(8,128)S(1)} %get-tuple-element.12.refs_0_, f32[512,128]{1,0:T(8,128)S(1)} %get-tuple-element.13.refs_1_, bf16[512,512]{1,0:T(8,128)(2,1)S(1)} %get-tuple-element.14.refs_2_, bf16[256,1664]{1,0:T(8,128)(2,1)S(1)} %collective-permute-done.refs_3_, ...), custom_call_target="tpu_custom_call" | custom-call | tf_op jit(solution)/shard_map/refine/pallas_call | solution.py:266
  53.6 16.3 %all_to_all.11 = f32[128,1,128]{2,1,0:T(1,128)S(1)} all-to-all(f32[128,1,128]{2,1,0:T(1,128)S(1)} %bitcast.9), channel_id=1, replica_groups=mesh['grp'=128,'rep'=2] {'grp'}, dimensions={0} | all-to-all | bytes 131072 | tf_op jit(solution)/shard_map/all_to_all | solution.py:336
  69.9 0.8 %pick.1 = f32[8,128]{1,0:T(8,128)} custom-call(f32[128,128]{1,0:T(8,128)S(1)} %bitcast.8, s32[8,128]{1,0:T(8,128)S(1)} %get-tuple-element.17.refs_1_), custom_call_target="tpu_custom_call" | custom-call | tf_op jit(solution)/shard_map/pick/pallas_call | solution.py:266
Async XLA Ops:
  3.5 44.9 %copy-start = (f32[512,768]{1,0:T(8,128)S(1)}, f32[512,768]{1,0:T(8,128)}, u32[]{:S(2)}) copy-start(f32[512,768]{1,0:T(8,128)} %refs_6_.1) | copy-start | bytes 4718596
  44.9 6.2 %collective-permute-start = (bf16[256,1664]{1,0:T(8,128)(2,1)S(1)}, bf16[256,1664]{1,0:T(8,128)(2,1)S(1)}, u32[]{:S(2)}, u32[]{:S(2)}) collective-permute-start(bf16[256,1664]{1,0:T(8,128)(2,1)S(1)} %reshape.21.got_ref.refs_5_), channel_id=1, source_target_pairs={{0,1},{1,0},{2,3},{3,2},{4,5},{5,4},{6,7},{7,6},{8,9},{9,8},{10,11... | collective-permute-start | bytes 2555912 | tf_op jit(solution)/shard_map/ppermute | solution.py:302
  49.9 1.3 %collective-permute-start.1 = (f32[8,512]{1,0:T(8,128)S(1)}, f32[8,512]{1,0:T(8,128)S(1)}, u32[]{:S(2)}, u32[]{:S(2)}) collective-permute-start(f32[8,512]{1,0:T(8,128)S(1)} %get-tuple-element.11.rows_ref), channel_id=1, source_target_pairs={{0,1},{1,0},{2,3},{3,2},{4,5},{5,4},{6,7},{7,6},{8,9},{9,8},{10,11... | collective-permute-start | bytes 49160 | tf_op jit(solution)/shard_map/ppermute | solution.py:310
